TPU v7x, 256 devices: a whole 4x4x8 slice. The times are simulated.
256 devices in a mesh: seq: 32 (over x_hi, z, core), zero: 8 (over x_lo, y).
Axes of the slice: x: 4 (x_hi: 2, x_lo: 2; x = x_hi * 2 + x_lo), y: 4, z: 8, core: 2. Of those that a mesh axis runs over, the one named last changes fastest.
Arguments:
- tokens: bfloat16 [8, 4096, 2048], P('zero', 'seq'), may hold values from -6 to 6
- w_in: bfloat16 [2048, 2336], P('zero'), may hold values from -0.0625 to 0.0625
- a_log: float32 [32], replicated, may hold values from -8 to 0
- dt_bias: float32 [32], replicated, may hold values from -4.5 to -3.5
- d_skip: float32 [32], replicated, may hold values from 0.5 to 1.5
- grad_y: bfloat16 [8, 4096, 2048], P('zero', 'seq'), may hold values from -6 to 6
Outputs:
- y_out: bfloat16 [8, 4096, 2048], P('zero', 'seq')
- grad_tokens: bfloat16 [8, 4096, 2048], P('zero', 'seq')
- grad_w: float32 [2048, 2336], P(('seq', 'zero'))
All inputs are finite; a program needn't handle non-finite values.
Results may differ from a plain program's by a relative error of at most 0.013.
Values may be sent and summed in bfloat16 or wider, within the bound.
A program may use at most 128 MiB of HBM per device.

v0:
```python
import jax
import jax.numpy as jnp
from jax import lax
from jax.sharding import Mesh
from jax.sharding import PartitionSpec as P

SEQ = ("seq_0", "seq_1", "seq_2")
SEQ_ZERO = ("seq_0", "seq_1", "seq_2", "zero")


def neutral_like(array, identity):
    return jax.tree.map(
        lambda a, e: jnp.broadcast_to(jnp.asarray(e, a.dtype), a.shape), array, identity
    )


def prefix_by_axis(array, axes, combine, identity, reverse):
    before = start = neutral_like(array, identity)
    so_far = array
    for axis in reversed(axes):
        size, position = (lax.axis_size(axis), lax.axis_index(axis))
        pieces = jax.tree.map(lambda part: lax.all_gather(part, axis), so_far)
        inside, so_far = (start, start)
        for k in reversed(range(size)) if reverse else range(size):
            passed = k > position if reverse else k < position
            so_far = combine(so_far, jax.tree.map(lambda part: part[k], pieces))
            inside = jax.tree.map(lambda new, old: jnp.where(passed, new, old), so_far, inside)
        before = combine(inside, before)
    return before


def cut_along(array, dim, size):
    before, after = (array.shape[:dim], array.shape[dim + 1 :])
    return jnp.moveaxis(array.reshape(*before, size, -1, *after), dim, 0)


def summed_on_arrival(array, axis, dim):
    size = lax.axis_size(axis)
    blocks = lax.all_to_all(cut_along(array, dim, size), axis, 0, 0, tiled=True)
    return jnp.sum(blocks, axis=0)


def block_ssd(xs, bm, cm, raw, start, a_log, dt_bias, d_skip):
    high = lax.Precision.DEFAULT
    dt = jax.nn.softplus(raw + dt_bias)
    loga = -jnp.exp(a_log) * dt
    cum = jnp.cumsum(loga, axis=0)
    count = xs.shape[0]
    later = (jnp.arange(count)[:, None] >= jnp.arange(count)[None, :])[:, :, None]
    spans = cum[:, None, :] - cum[None, :, :]
    decay = jnp.where(later, jnp.exp(jnp.where(later, spans, 0.0)), 0.0)
    scores = jnp.dot(cm, bm.T, precision=high)
    mixing = scores[:, :, None] * decay * dt[None, :, :]
    ssd = jnp.einsum("tsh,shp->thp", mixing, xs, precision=high)
    ssd = ssd + jnp.einsum("tn,th,hpn->thp", cm, jnp.exp(cum), start, precision=high)
    out = ssd + d_skip[None, :, None] * xs
    tail = jnp.exp(cum[-1:] - cum) * dt
    state = jnp.exp(cum[-1])[:, None, None] * start + jnp.einsum(
        "sh,sn,shp->hpn", tail, bm, xs, precision=high
    )
    return (out, state)


def carry_forward(earlier, later):
    return (earlier[0] + later[0], jnp.exp(later[0])[:, None, None] * earlier[1] + later[1])


def carry_backward(earlier, later):
    return (earlier[0] + later[0], later[1] + jnp.exp(later[0])[:, None, None] * earlier[1])


def rounded(values):
    return lax.optimization_barrier(values.astype(jnp.bfloat16)).astype(jnp.float32)


def per_device(tokens, w_in, a_log, dt_bias, d_skip, grad_y):
    high = lax.Precision.DEFAULT
    count = tokens.shape[1]
    width = tokens.shape[2]
    inner = grad_y.shape[2]
    heads = a_log.shape[0]
    head_width = inner // heads
    state_width = (w_in.shape[1] - inner - heads) // 2
    columns_all = w_in.shape[1]
    rows = tokens.reshape(count, width)
    full_w = lax.all_gather(w_in, "zero", axis=0, tiled=True)
    proj = jnp.dot(rows, full_w, preferred_element_type=jnp.float32)
    xs = rounded(proj[:, :inner]).reshape(count, heads, head_width)
    bm = rounded(proj[:, inner : inner + state_width])
    cm = rounded(proj[:, inner + state_width : inner + 2 * state_width])
    raw = proj[:, inner + 2 * state_width :]
    dt = jax.nn.softplus(raw + dt_bias)
    cum = jnp.cumsum(-jnp.exp(a_log) * dt, axis=0)
    total = cum[-1]
    empty_state = jnp.zeros((heads, head_width, state_width), jnp.float32)
    empty_total = jnp.zeros((heads,), jnp.float32)
    local_out, local_state = block_ssd(xs, bm, cm, raw, empty_state, a_log, dt_bias, d_skip)
    prior = prefix_by_axis(
        (total, local_state), SEQ, carry_forward, (empty_total, empty_state), False
    )
    start_state = prior[1]
    growth = jnp.exp(cum)
    outputs = local_out + jnp.einsum("tn,th,hpn->thp", cm, growth, start_state, precision=high)
    y_out = outputs.reshape(1, count, inner).astype(jnp.bfloat16)
    cotangent = grad_y.reshape(count, heads, head_width).astype(jnp.float32)
    back_local = jnp.einsum("tn,th,thp->hpn", cm, growth, cotangent, precision=high)
    after = prefix_by_axis(
        (total, back_local), SEQ, carry_backward, (empty_total, empty_state), True
    )
    end_adjoint = after[1]

    def local_layer(xin, bin_, cin, rin, sin):
        return block_ssd(xin, bin_, cin, rin, sin, a_log, dt_bias, d_skip)

    unused, pullback = jax.vjp(local_layer, xs, bm, cm, raw, start_state)
    grad_x, grad_b, grad_c, grad_raw, unused_state = pullback((cotangent, end_adjoint))
    gproj = jnp.concatenate(
        [grad_x.reshape(count, inner), grad_b, grad_c, grad_raw], axis=1
    ).astype(jnp.bfloat16)
    grad_rows = lax.dot_general(
        gproj, full_w, (((1,), (1,)), ((), ())), preferred_element_type=jnp.float32
    )
    grad_tokens = grad_rows.astype(jnp.bfloat16).reshape(1, count, width)
    seq_count = lax.axis_size(SEQ)
    zero_count = lax.axis_size("zero")
    piece = width // (seq_count * zero_count)
    owned = width // zero_count
    permuted = (
        rows.reshape(count, seq_count, zero_count, piece)
        .transpose(0, 2, 1, 3)
        .reshape(count, width)
    )
    received = lax.all_to_all(permuted, "zero", split_axis=1, concat_axis=0, tiled=True)
    pieces = lax.all_gather(gproj, "zero", axis=0, tiled=True)
    length = pieces.shape[0]
    shards = length // count
    parts = jnp.einsum(
        "ktr,kte->kre",
        received.reshape(shards, count, owned),
        pieces.reshape(shards, count, columns_all),
        preferred_element_type=jnp.float32,
    )
    zero_rows = jnp.sum(rounded(parts), axis=0)
    grad_w = summed_on_arrival(zero_rows, SEQ, 0)
    return (y_out, grad_tokens, grad_w)


def solution(mesh):
    torus = Mesh(
        mesh.devices.reshape(2, 8, 2, mesh.shape["zero"]), ("seq_0", "seq_1", "seq_2", "zero")
    )
    placed = (P("zero", SEQ, None), P("zero", None), P(), P(), P(), P("zero", SEQ, None))
    return jax.shard_map(
        per_device,
        mesh=torus,
        in_specs=placed,
        out_specs=(P("zero", SEQ, None), P("zero", SEQ, None), P(SEQ_ZERO, None)),
        check_vma=False,
    )
```

profile of v0, /device:TPU:1, one launch (start us, length us, event | category | flops | bytes accessed | tf_op | source)
XLA Modules:
  0.0 611.0 jit_solution(15734096874288468262)
XLA Ops:
  7.2 0.7 all-gather.15.cloned.1.call-update
  7.9 0.7 exponential_negate_fusion
  8.6 111.9 %all-gather.15.cloned.1.call-done = bf16[2048,2336]{0,1:T(8,128)(2,1)} async-done(((bf16[256,2336]{0,1:T(8,128)(2,1)}), bf16[2048,2336]{0,1:T(8,128)(2,1)}) %all-gather.15.cloned.1.call-update) | async-done | bytes 9568272 | tf_op jit(solution)/shard_map/all_gather | solution.py:86
  120.5 5.4 fusion.118
  126.0 0.1 copy.153
  126.1 0.2 reduce_window_sum.25
  126.4 0.1 fusion.82
  126.5 0.1 copy.116
  126.5 1.3 convolution_add_fusion
  128.0 0.3 copy.119
  128.2 0.1 copy.114
  128.3 1.3 fusion.29
  129.7 5.1 all-gather.2
  134.8 13.4 %all-gather.27.cloned.1.call-done = f32[64,64,128]{2,1,0:T(8,128)} async-done(((f32[32,64,128]{2,1,0:T(8,128)}), f32[64,64,128]{2,1,0:T(8,128)}) %all-gather.27.cloned.1.call-update) | async-done | bytes 2097168 | tf_op jit(solution)/shard_map/all_gather | solution.py:22
  148.1 2.7 bitcast_add_fusion.17
  151.0 16.2 %all-gather.29.cloned.1.call-done = f32[64,64,128]{2,1,0:T(8,128)} async-done(((f32[32,64,128]{2,1,0:T(8,128)}), f32[64,64,128]{2,1,0:T(8,128)}) %all-gather.29.cloned.1.call-update) | async-done | bytes 2097168 | tf_op jit(solution)/shard_map/all_gather | solution.py:22
  167.2 2.8 fusion.53
  170.0 12.6 %all-gather.3 = f32[8,1,32]{2,1,0:T(1,128)S(1)} all-gather(f32[1,1,32]{2,1,0:T(1,128)S(1)} %get-tuple-element.61), channel_id=1, replica_groups=mesh['seq_0'=2,'seq_1'=8,'seq_2'=2,'zero'=8] {'seq_1'}, dimensions={0}, use_global_device_ids=true | all-gather | bytes 1152 | tf_op jit(solution)/shard_map/all_gather | solution.py:22
  182.6 80.7 %all-gather.17.cloned.1.call-done = f32[8,32,64,128]{3,2,1,0:T(8,128)} async-done(((f32[1,32,64,128]{3,2,1,0:T(8,128)}), f32[8,32,64,128]{3,2,1,0:T(8,128)}) %all-gather.17.cloned.1.call-update) | async-done | bytes 8388624 | tf_op jit(solution)/shard_map/all_gather | solution.py:22
  263.3 4.5 multiply_add_fusion.1
  268.0 89.7 %all-gather.21.cloned.1.call-done = f32[8,32,64,128]{3,2,1,0:T(8,128)} async-done(((f32[1,32,64,128]{3,2,1,0:T(8,128)}), f32[8,32,64,128]{3,2,1,0:T(8,128)}) %all-gather.21.cloned.1.call-update) | async-done | bytes 8388624 | tf_op jit(solution)/shard_map/all_gather | solution.py:22
  357.7 4.7 multiply_add_fusion
  362.7 4.6 all-gather.4
  367.3 4.8 all-gather.5
  372.0 0.8 fusion.119
  372.9 24.8 %all-gather.19.cloned.1.call-done = f32[2,32,64,128]{3,2,1,0:T(8,128)} async-done(((f32[1,32,64,128]{3,2,1,0:T(8,128)}), f32[2,32,64,128]{3,2,1,0:T(8,128)}) %all-gather.19.cloned.1.call-update) | async-done | bytes 2097168 | tf_op jit(solution)/shard_map/all_gather | solution.py:22
  397.6 41.0 %all-gather.23.cloned.1.call-done = f32[2,32,64,128]{3,2,1,0:T(8,128)} async-done(((f32[1,32,64,128]{3,2,1,0:T(8,128)}), f32[2,32,64,128]{3,2,1,0:T(8,128)}) %all-gather.23.cloned.1.call-update) | async-done | bytes 2097168 | tf_op jit(solution)/shard_map/all_gather | solution.py:22
  438.6 10.4 %multiply_reduce_fusion.1 = (f32[32]{0:T(128)}, bf16[32,64,128]{2,1,0:T(8,128)(2,1)S(1)}, bf16[32,64,128]{2,1,0:T(8,128)(2,1)S(1)}) fusion(pred[]{:T(512)S(6)} %lt.47, f32[32]{0:T(128)S(1)} %get-tuple-element.63, f32[2,32,64,128]{3,2,1,0:T(8,128)} %all-gather.23.cloned.1.call-done, f32[32]{0:T(128)S(1)} %get-tuple-element.62, pred[]{:T(512)S(6)} %lt.46, ...), kind=kLoop, calls=%fused_computation.90 | loop fusion | flops 20447200 | bytes 26217368 | tf_op jit(solution)/shard_map/transpose(jvp())/reduce_sum | solution.py:58
  449.0 0.3 fusion.36
  449.3 0.3 fusion.30
  449.7 0.3 convolution_bitcast_fusion.1
  450.0 1.3 fusion.38
  451.3 0.1 copy.141
  451.4 0.1 fusion.111
  451.6 2.0 fusion.34
  453.7 0.1 fusion.31
  453.8 0.1 fusion.32
  454.0 0.1 copy.123
  454.1 0.1 copy.124
  454.2 0.1 copy.147
  454.3 0.1 add_add_fusion
  454.4 1.1 reduce_window_sum.26
  455.5 0.1 copy.122
  455.6 0.1 fusion.81
  455.7 0.1 copy.125
  455.8 1.9 fusion.23
  457.8 0.9 pad_maximum_fusion
  458.7 0.5 copy-done.2
  459.2 0.3 copy.126
  459.4 0.1 copy.160
  459.6 0.2 copy.128
  459.8 12.3 %all_to_all.21 = bf16[128,8,256]{2,0,1:T(8,128)(2,1)S(1)} all-to-all(bf16[128,8,256]{2,0,1:T(8,128)(2,1)S(1)} %copy.128), channel_id=1, replica_groups=mesh['seq_0'=2,'seq_1'=8,'seq_2'=2,'zero'=8] {'zero'}, dimensions={1} | all-to-all | bytes 1048576 | tf_op jit(solution)/shard_map/all_to_all | solution.py:133
  472.1 50.4 %all-gather.25.cloned.1.call-done = bf16[1024,2336]{0,1:T(8,128)(2,1)} async-done(((bf16[128,2336]{0,1:T(8,128)(2,1)}), bf16[1024,2336]{0,1:T(8,128)(2,1)}) %all-gather.25.cloned.1.call-update) | async-done | bytes 4784144 | tf_op jit(solution)/shard_map/all_gather | solution.py:134
  522.5 5.0 convert_bitcast_fusion
  527.5 1.3 convert_reduce_fusion
  528.8 2.0 copy.130
  530.9 13.0 %all-to-all-start.1 = ((f32[32,8,2336]{2,1,0:T(8,128)}), f32[32,8,2336]{2,1,0:T(8,128)S(1)}, u32[]{:S(2)}, u32[]{:S(2)}) async-start(f32[32,8,2336]{2,1,0:T(8,128)} %bitcast.397), calls=%async_computation.1 | async-start | bytes 4980736 | tf_op jit(solution)/shard_map/all_to_all | solution.py:39
  543.9 0.9 fusion.11
  544.8 0.3 copy-done.1
  545.1 1.2 fusion.26
  546.3 2.0 copy.131
  548.4 6.1 %fusion.2 = bf16[1,128,2048]{2,1,0:T(8,128)(2,1)} fusion(bf16[2048,2336]{0,1:T(8,128)(2,1)} %all-gather.15.cloned.1.call-done, bf16[128,32]{0,1:T(8,128)(2,1)} %copy-done.10, bf16[128,128]{0,1:T(8,128)(2,1)} %copy-done.9, bf16[128,128]{0,1:T(8,128)(2,1)} %copy-done.8, bf16[128,2048]{0,1:T(8,128)(2,1)S(1)} %bitcast.410), kind=kOutput, calls=%fused_computation.5 | convolution fusion | flops 1227390976 | bytes 10690560 | tf_op jit(solution)/shard_map/dot_general | solution.py:120
  554.5 48.9 %all-to-all-done.1 = f32[32,8,2336]{2,1,0:T(8,128)S(1)} async-done(((f32[32,8,2336]{2,1,0:T(8,128)}), f32[32,8,2336]{2,1,0:T(8,128)S(1)}, u32[]{:S(2)}, u32[]{:S(2)}) %all-to-all-start.1) | async-done | bytes 2392096 | tf_op jit(solution)/shard_map/all_to_all | solution.py:39
  603.4 0.8 reduce_sum.86
  (88 shorter events, 1.0 us)
Async XLA Ops:
  7.2 113.4 %all-gather.15.cloned.1.call-start = ((), (), s32[]{:S(2)}) async-start(), calls=%async_computation.2 | async-start | bytes 10764288 | tf_op jit(solution)/shard_map/all_gather | solution.py:86
  7.9 140.2 %all-gather.27.cloned.1.call-start = ((), (), s32[]{:S(2)}) async-start(), calls=%async_computation.8 | async-start | bytes 3145728 | tf_op jit(solution)/shard_map/all_gather | solution.py:22
  8.6 117.5 %copy-start.23 = (f32[32]{0:T(128)}, f32[32]{0:T(128)S(1)}, u32[]{:S(2)}) copy-start(f32[32]{0:T(128)S(1)} %exponential_negate_fusion) | copy-start | bytes 388
  8.6 117.5 %copy-start.19 = (f32[32]{0:T(128)S(1)}, f32[32]{0:T(128)}, u32[]{:S(2)}) copy-start(f32[32]{0:T(128)} %param.9) | copy-start | bytes 388
  126.3 1.6 copy-start.21
  126.3 1.6 copy-start.7
  126.4 327.3 %copy-start.5 = (bf16[128,128]{0,1:T(8,128)(2,1)}, bf16[128,128]{0,1:T(8,128)(2,1)S(1)}, u32[]{:S(2)}) copy-start(bf16[128,128]{0,1:T(8,128)(2,1)S(1)} %get-tuple-element.34) | copy-start | bytes 98308
  127.9 39.3 %all-gather.29.cloned.1.call-start = ((), (), s32[]{:S(2)}) async-start(), calls=%async_computation.9 | async-start | bytes 3145728 | tf_op jit(solution)/shard_map/all_gather | solution.py:22
  129.6 133.7 %all-gather.17.cloned.1.call-start = ((), (), s32[]{:S(2)}) async-start(), calls=%async_computation.3 | async-start | bytes 9437184 | tf_op jit(solution)/shard_map/all_gather | solution.py:22
  150.9 206.8 %all-gather.21.cloned.1.call-start = ((), (), s32[]{:S(2)}) async-start(), calls=%async_computation.5 | async-start | bytes 9437184 | tf_op jit(solution)/shard_map/all_gather | solution.py:22
  170.0 227.7 %all-gather.19.cloned.1.call-start = ((), (), s32[]{:S(2)}) async-start(), calls=%async_computation.4 | async-start | bytes 3145728 | tf_op jit(solution)/shard_map/all_gather | solution.py:22
  267.9 170.7 %all-gather.23.cloned.1.call-start = ((), (), s32[]{:S(2)}) async-start(), calls=%async_computation.6 | async-start | bytes 3145728 | tf_op jit(solution)/shard_map/all_gather | solution.py:22
  357.7 80.9 %copy-start = (f32[64,64,128]{2,1,0:T(8,128)S(1)}, f32[64,64,128]{2,1,0:T(8,128)}, u32[]{:S(2)}) copy-start(f32[64,64,128]{2,1,0:T(8,128)} %all-gather.27.cloned.1.call-done) | copy-start | bytes 6291460
  362.4 160.1 %all-gather.25.cloned.1.call-start = ((), (), s32[]{:S(2)}) async-start(), calls=%async_computation.7 | async-start | bytes 5382144 | tf_op jit(solution)/shard_map/all_gather | solution.py:134
  362.5 89.0 %copy-start.17 = (pred[128,128]{1,0:T(8,128)(4,1)}, pred[128,128]{1,0:T(8,128)(4,1)S(1)}, u32[]{:S(2)}) copy-start(pred[128,128]{1,0:T(8,128)(4,1)S(1)} %iota_compare_fusion) | copy-start | bytes 49156
  362.6 89.0 %copy-start.13 = (f32[128,32]{0,1:T(8,128)}, f32[128,32]{0,1:T(8,128)S(1)}, u32[]{:S(2)}) copy-start(f32[128,32]{0,1:T(8,128)S(1)} %copy.111) | copy-start | bytes 49156
  449.3 2.1 copy-start.20
  449.3 2.1 copy-start.22
  449.7 1.9 copy-start.11
  451.5 4.3 copy-start.15
  451.6 2.7 copy-start.25
  451.6 4.0 copy-start.24
  451.6 4.2 copy-start.26
  453.8 3.9 copy-start.8
  454.0 3.8 copy-start.9
  455.8 2.0 copy-start.10
  457.7 2.0 copy-start.3
  457.7 1.4 copy-start.2
  530.8 13.0 %copy-start.12 = (f32[128,128]{1,0:T(8,128)S(1)}, f32[128,128]{1,0:T(8,128)}, u32[]{:S(2)}) copy-start(f32[128,128]{1,0:T(8,128)} %fusion.119) | copy-start | bytes 196612
  530.8 13.0 %copy-start.14 = (f32[128,32]{0,1:T(8,128)S(1)}, f32[128,32]{0,1:T(8,128)}, u32[]{:S(2)}) copy-start(f32[128,32]{0,1:T(8,128)} %copy-done.13) | copy-start | bytes 49156
  530.9 13.0 %copy-start.16 = (f32[128,32]{0,1:T(8,128)S(1)}, f32[128,32]{0,1:T(8,128)}, u32[]{:S(2)}) copy-start(f32[128,32]{0,1:T(8,128)} %copy-done.15) | copy-start | bytes 49156
  530.9 13.0 %copy-start.18 = (pred[128,128]{1,0:T(8,128)(4,1)S(1)}, pred[128,128]{1,0:T(8,128)(4,1)}, u32[]{:S(2)}) copy-start(pred[128,128]{1,0:T(8,128)(4,1)} %copy-done.17) | copy-start | bytes 49156
  530.9 72.5 %all-to-all-start.1 = ((f32[32,8,2336]{2,1,0:T(8,128)}), f32[32,8,2336]{2,1,0:T(8,128)S(1)}, u32[]{:S(2)}, u32[]{:S(2)}) async-start(f32[32,8,2336]{2,1,0:T(8,128)} %bitcast.397), calls=%async_computation.1 | async-start | bytes 4980736 | tf_op jit(solution)/shard_map/all_to_all | solution.py:39
  543.9 1.2 copy-start.1
  543.9 1.2 copy-start.6
  543.9 1.2 copy-start.27
  545.1 3.3 copy-start.4
Sparse Core Ops, SparseCore 0:
  9.7 110.8 all-gather.14
  128.0 20.0 all-gather.26
  149.9 17.1 all-gather.28
  168.8 94.4 all-gather.16
  265.0 92.6 all-gather.20
  359.3 38.2 all-gather.18
  399.4 39.1 all-gather.22
  458.8 63.6 all-gather.24
where the time goes:
time: 612 us; the launch traced here: 611 us
  waiting for transfers between devices  478 us (78%)
  blocking collectives  39.3 us (6%)
  other arithmetic  30.6 us (5%)
  matrix products  28.6 us (5%)
  between operations  14.7 us (2%)
  starting transfers between devices  13.3 us (2%)
  local copies, waits for them, and re-layouts  6.76 us (1%)
    all_gather x6, waiting for transfers between devices, prefix_by_axis(): pieces = jax.tree.map(lambda part: lax.all_gather(part, axis), so_far)  266 us
    all_gather x1, waiting for transfers between devices, per_device(): full_w = lax.all_gather(w_in, 'zero', axis=0, tiled=True)  112 us
    all_gather x1, waiting for transfers between devices, per_device(): pieces = lax.all_gather(gproj, 'zero', axis=0, tiled=True)  50.4 us
    all_to_all x1, waiting for transfers between devices, summed_on_arrival(): blocks = lax.all_to_all(cut_along(array, dim, size), axis, 0, 0, tiled=True)  48.9 us
    all_gather x4, blocking collectives, prefix_by_axis(): pieces = jax.tree.map(lambda part: lax.all_gather(part, axis), so_far)  27 us
    all_to_all x1, starting transfers between devices, summed_on_arrival(): blocks = lax.all_to_all(cut_along(array, dim, size), axis, 0, 0, tiled=True)  13 us
    all_to_all x1, blocking collectives, per_device(): lax.all_to_all(permuted, 'zero', split_axis=1, concat_axis=0, tiled=True)  12.3 us
  transfers between devices with their start and end apart: 9, of which 9 were waited for; matrix products, arithmetic and copies ran while one was open for 5% of the time, Pallas kernels for 0%

commit v1 on v0

v1 whole, which is shorter than its diff:
```python
import jax
import jax.numpy as jnp
from jax import lax
from jax.experimental import pallas as pl
from jax.experimental.pallas import tpu as pltpu
from jax.sharding import Mesh
from jax.sharding import PartitionSpec as P

SEQ = ("xh", "z", "c")
ZERO = ("xl", "y")
MESH = pl.DeviceIdType.MESH
F32 = jnp.float32
BF16 = jnp.bfloat16
LIMIT = 60 * 1024 * 1024
VM = pl.BlockSpec(memory_space=pltpu.VMEM)
ANY = pl.BlockSpec(memory_space=pl.ANY)


def remote(src, dst, send, recv, target):
    return pltpu.make_async_remote_copy(
        src_ref=src, dst_ref=dst, send_sem=send, recv_sem=recv, device_id=target, device_id_type=MESH
    )


def greet(targets):
    barrier = pltpu.get_barrier_semaphore()
    for target in targets:
        pl.semaphore_signal(barrier, inc=1, device_id=target, device_id_type=MESH)
    pl.semaphore_wait(barrier, len(targets))


def place():
    return tuple(lax.axis_index(a) for a in ("xh", "z", "c", "xl", "y"))


def along_x(x):
    return {"xh": x // 2, "xl": x % 2}


def dot(a, b, precision=None):
    return jnp.dot(a, b, preferred_element_type=F32, precision=precision)


def dot_nt(a, b):
    return lax.dot_general(a, b, (((1,), (1,)), ((), ())), preferred_element_type=F32)


def gather_kernel(tok, w, x_o, bc_o, raw_o, wf_o, t1_o, t2_o, wbuf, acc, tt, tb, tr, ici_s, ici_r, d2d_s, d2d_r, tok_sem, hbm_sem, own_sem):
    xh, z, c, xl, y = place()
    x = xh * 2 + xl
    right, left = along_x((x + 1) % 4), along_x((x + 3) % 4)
    up, down = {"y": (y + 1) % 4}, {"y": (y + 3) % 4}
    mate = {"c": 1 - c}
    greet((mate, right, left, up, down))
    inner = x_o.shape[1]
    depth = w.shape[0]
    piece = depth // 4
    sends = []

    def shard(flip, dy):
        return (xl + flip) % 2 * 4 + (y + dy) % 4

    rel = [shard(0, 3), shard(0, 1), shard(0, 2), shard(1, 0), shard(1, 3), shard(1, 1), shard(1, 2)]
    mine = shard(0, 0)

    def rows(core, part):
        return pl.ds(pl.multiple_of((core * 2 + part) * piece, piece), piece)

    def send(k, part, to, slot, src=None):
        block = wbuf.at[k, rows(c, part)]
        n = len(sends)
        copy = remote(block if src is None else src, block, ici_s.at[n], ici_r.at[slot, part], to)
        copy.start()
        sends.append(copy)

    own = [w.at[rows(c, part)] for part in range(2)]
    send(mine, 0, up, 0, own[0])
    send(mine, 1, down, 1, own[1])
    send(mine, 0, left, 3, own[0])
    send(mine, 1, right, 3, own[1])
    send(mine, 1, up, 0, own[1])
    send(mine, 0, down, 1, own[0])
    local = pltpu.make_async_copy(w, wbuf.at[mine], own_sem)
    local.start()

    for i in range(16):
        block = tok[:, i * 128 : (i + 1) * 128].astype(F32).T
        for r in range(16):
            core, xlow, yy = r // 8, r // 4 % 2, r % 4
            tt[core, i // 8 * 2 + xlow, yy, i % 8 * 8 : i % 8 * 8 + 8, :] = block[r * 8 : r * 8 + 8, :]
    tb[...] = tt[...].astype(BF16)
    swap = remote(tb.at[1 - c], tr, tok_sem.at[0], tok_sem.at[1], mate)
    swap.start()
    half = tb[pl.ds(c, 1)][0]
    t1_o[:, :, :, :128] = half
    for a in range(4):
        for b in range(4):
            t2_o[b, a, :, :128] = half[a, b]
    acc[...] = jnp.zeros_like(acc)
    local.wait()

    outs = []

    def out(k):
        copy = pltpu.make_async_copy(wbuf.at[k], wf_o.at[k], hbm_sem.at[len(outs)])
        copy.start()
        outs.append(copy)

    def arrive(slot, part):
        k = rel[slot]
        block = wbuf.at[k, rows(c, part)]
        remote(block, block, ici_s.at[0], ici_r.at[slot, part], mate).wait_recv()
        copy = remote(block, block, d2d_s.at[slot, part], d2d_r.at[slot, part], mate)
        copy.start()
        sends.append(copy)

    def whole(slot):
        for part in range(2):
            block = wbuf.at[rel[slot], rows(1 - c, part)]
            remote(block, block, d2d_s.at[slot, part], d2d_r.at[slot, part], mate).wait_recv()
        out(rel[slot])

    def forward(slot, part, to, there):
        k = rel[slot]
        block = wbuf.at[k, rows(c, part)]
        copy = remote(block, block, ici_s.at[count[0]], ici_r.at[there, part], to)
        count[0] += 1
        copy.start()
        sends.append(copy)

    count = [len(sends)]

    def multiply(ks):
        def body(i, carry):
            k = ks[0]
            for n in range(1, len(ks)):
                k = jnp.where(i == n, ks[n], k)
            acc[...] += dot(tok[:, pl.ds(pl.multiple_of(k * depth, depth), depth)], wbuf[k])
            return carry

        lax.fori_loop(0, len(ks), body, 0)

    out(mine)
    multiply([mine])
    arrive(0, 0)
    forward(0, 0, up, 2)
    forward(0, 0, left, 4)
    arrive(1, 1)
    forward(1, 1, down, 2)
    forward(1, 1, right, 5)
    arrive(3, 0)
    arrive(3, 1)
    arrive(0, 1)
    forward(0, 1, right, 4)
    arrive(1, 0)
    forward(1, 0, left, 5)
    arrive(4, 0)
    arrive(5, 1)
    whole(3)
    whole(0)
    whole(1)
    multiply([rel[3], rel[0], rel[1]])
    arrive(2, 0)
    forward(2, 0, left, 6)
    arrive(2, 1)
    forward(2, 1, right, 6)
    arrive(4, 1)
    arrive(5, 0)
    whole(2)
    whole(4)
    whole(5)
    multiply([rel[2], rel[4], rel[5]])
    swap.wait()
    other = tr[...]
    t1_o[:, :, :, 128:] = other
    for a in range(4):
        for b in range(4):
            t2_o[b, a, :, 128:] = other[a, b]
    arrive(6, 0)
    arrive(6, 1)
    whole(6)
    multiply([rel[6]])
    x_o[...] = acc[:, :inner].astype(BF16)
    wide = bc_o.shape[1]
    bc_o[...] = acc[:, inner : inner + wide].astype(BF16)
    raw_o[...] = acc[:, inner + wide :]
    for copy in sends:
        copy.wait_send()
    for copy in outs:
        copy.wait()


def gather(tokens, w):
    count, width = tokens.shape
    depth, cols = w.shape
    sd = jax.ShapeDtypeStruct
    return pl.pallas_call(
        gather_kernel,
        out_shape=(
            sd((count, 2048), BF16),
            sd((count, 256), BF16),
            sd((count, 32), F32),
            sd((8, depth, cols), BF16),
            sd((4, 4, 64, 2 * count), BF16),
            sd((4, 4, 64, 2 * count), BF16),
        ),
        in_specs=[VM, VM],
        out_specs=(VM, VM, VM, ANY, VM, VM),
        scratch_shapes=[
            pltpu.VMEM((8, depth, cols), BF16),
            pltpu.VMEM((count, cols), F32),
            pltpu.VMEM((2, 4, 4, 64, count), F32),
            pltpu.VMEM((2, 4, 4, 64, count), BF16),
            pltpu.VMEM((4, 4, 64, count), BF16),
            pltpu.SemaphoreType.DMA((14,)),
            pltpu.SemaphoreType.DMA((7, 2)),
            pltpu.SemaphoreType.DMA((7, 2)),
            pltpu.SemaphoreType.DMA((7, 2)),
            pltpu.SemaphoreType.DMA((2,)),
            pltpu.SemaphoreType.DMA((8,)),
            pltpu.SemaphoreType.DMA,
        ],
        compiler_params=pltpu.CompilerParams(collective_id=0, has_side_effects=True, vmem_limit_bytes=LIMIT),
    )(tokens, w)


def spread(row):
    lane = lax.broadcasted_iota(jnp.int32, (row.shape[0], 128), 1)
    out = []
    for j in range(16):
        out.append(jnp.where(lane < 64, row[:, 2 * j : 2 * j + 1], row[:, 2 * j + 1 : 2 * j + 2]))
    return out


def scan_kernel(
    x_r, bc_r, raw_r, al_r, bias_r, skip_r, g_r, y_o, ga_o, gb_o,
    dte, ece, tle, cume, cumt, xdt, xt, gec, yi, dxi, ds_acc,
    stf, sst, pst, tot_s, tot_r, te, msg, rmsg, dmsg, dr, res, rres, se, hs, ske,
    d_sem, s0, r0, s1, r1, s2, r2,
):
    xh, z, c, xl, y = place()
    chip = xh * 8 + z
    mate = {"c": 1 - c}
    others = []
    for d in range(1, 16):
        t = (chip + d) % 16
        others.append((d, t, (chip + 16 - d) % 16, {"xh": t // 8, "z": t % 8}))
    greet([mate] + [o[3] for o in others])

    count = x_r.shape[0]
    zeros = jnp.zeros((count, 96), F32)
    rowz = jnp.zeros((1, 96), F32)
    decay_rate = jnp.concatenate([-jnp.exp(al_r[...]), rowz], axis=1)
    bias = jnp.concatenate([bias_r[...], rowz], axis=1)
    u = jnp.concatenate([raw_r[...], zeros], axis=1) + bias
    small = jnp.exp(-jnp.abs(u))
    dt = jnp.maximum(u, 0.0) + jnp.log1p(small)
    sig = jnp.where(u >= 0, 1.0, small) / (1.0 + small)
    ti = lax.broadcasted_iota(jnp.int32, (128, 128), 0)
    si = lax.broadcasted_iota(jnp.int32, (128, 128), 1)
    keep = ti >= si
    keep_t = ti <= si
    lower = jnp.where(keep, 1.0, 0.0).astype(F32)
    upper = jnp.where(keep_t, 1.0, 0.0).astype(F32)
    cum = dot(lower, decay_rate * dt, lax.Precision.HIGHEST)
    total = cum[127:128, :]
    tot_s[...] = jnp.broadcast_to(total, (8, 128))
    tot_copy = remote(tot_s, tot_r, d_sem.at[0], d_sem.at[1], mate)
    tot_copy.start()
    growth = jnp.exp(cum)
    tail = jnp.exp(total - cum)
    cumt[...] = cum.T
    lane = lax.broadcasted_iota(jnp.int32, (count, 128), 1)
    for arr, dst in ((dt, dte), (growth, ece), (tail, tle)):
        for j, e in enumerate(spread(arr)):
            dst[:, j * 128 : (j + 1) * 128] = e
    for j, e in enumerate(spread(jnp.broadcast_to(jnp.concatenate([skip_r[...], rowz], axis=1), (8, 128)))):
        ske[:, j * 128 : (j + 1) * 128] = e
    xf = x_r[...].astype(F32)
    gf = g_r[...].astype(F32)
    xd = xf * dte[...]
    xdt[...] = xd.astype(BF16)
    xt[...] = (xd * tle[...]).astype(BF16)
    gec[...] = (gf * ece[...]).astype(BF16)
    bm = bc_r[:, :128]
    cm = bc_r[:, 128:]
    bt = bm.astype(F32).T.astype(BF16)
    ct = cm.astype(F32).T.astype(BF16)
    for half in range(2):
        cols = slice(half * 1024, half * 1024 + 1024)
        stf[half, 0] = dot(bt, xt[:, cols])
        stf[half, 1] = dot(ct, gec[:, cols])
    sst[...] = stf[pl.ds(1 - c, 1)][0].astype(BF16)
    st_copy = remote(sst, pst, d_sem.at[2], d_sem.at[3], mate)
    st_copy.start()
    tot_copy.wait()
    for n, arr in enumerate((tot_s, tot_r)):
        for j, e in enumerate(spread(arr[...])):
            te[n, j // 8, :, j % 8 * 128 : j % 8 * 128 + 128] = e
    t_own = te[0, pl.ds(c, 1)][0][0:1]
    t_mate = te[1, pl.ds(c, 1)][0][0:1]
    first = c == 0
    for j in range(8):
        dmsg[j] = te[0, pl.ds(c, 1), :, j * 128 : j * 128 + 128][0] + te[1, pl.ds(c, 1), :, j * 128 : j * 128 + 128][0]
    dr[pl.ds(chip, 1)] = dmsg[pl.ds(chip // 2, 1)]
    copies = []
    for d, t, source, target in others:
        copy = remote(dmsg.at[t // 2], dr.at[chip], s0.at[d], r0.at[d], target)
        copy.start()
        copies.append(copy)
    e_own, e_mate = jnp.exp(t_own), jnp.exp(t_mate)
    e0 = jnp.where(first, e_own, e_mate)
    e1 = jnp.where(first, e_mate, e_own)
    st_copy.wait()
    own_f, own_b = stf[pl.ds(c, 1), 0][0], stf[pl.ds(c, 1), 1][0]
    mate_f, mate_b = pst[0].astype(F32), pst[1].astype(F32)
    f0 = jnp.where(first, own_f, mate_f)
    f1 = jnp.where(first, mate_f, own_f)
    b0 = jnp.where(first, own_b, mate_b)
    b1 = jnp.where(first, mate_b, own_b)
    chip_f = (e1 * f0 + f1).astype(BF16)
    chip_b = (b0 + e0 * b1).astype(BF16)
    for i in range(16):
        r, l = slice(i % 2 * 64, i % 2 * 64 + 64), slice(i // 2 * 128, i // 2 * 128 + 128)
        msg[i, 0] = chip_f[r, l]
        msg[i, 1] = chip_b[r, l]
    for d, t, source, target in others:
        copy = remote(msg.at[t], rmsg.at[chip], s1.at[d], r1.at[d], target)
        copy.start()
        copies.append(copy)
    rmsg[pl.ds(chip, 1)] = msg[pl.ds(chip, 1)]

    scores = dot_nt(cm, bm)
    scores_t = dot_nt(bm, cm)
    ds_acc[...] = jnp.zeros_like(ds_acc)
    for h in range(32):
        cume[:, h * 128 : h * 128 + 128] = jnp.broadcast_to(cum[:, h : h + 1], (count, 128))

    def pair(j, carry):
        cols = pl.ds(pl.multiple_of(j * 128, 128), 128)
        lows = pl.ds(pl.multiple_of(j * 256, 128), 128)
        highs = pl.ds(pl.multiple_of(j * 256 + 128, 128), 128)
        xj = xdt[:, cols]
        gj = g_r[:, cols]
        none = jnp.zeros_like(xj)
        xx = jnp.concatenate([jnp.where(lane < 64, xj, none), jnp.where(lane < 64, none, xj)], axis=0)
        gg = jnp.concatenate([jnp.where(lane < 64, gj, none), jnp.where(lane < 64, none, gj)], axis=0)
        ww = dot_nt(gg, xj)
        mix, mix_t = [], []
        total_ds = ds_acc[...]
        for n, where in enumerate((lows, highs)):
            span = cume[:, where] - cumt[pl.ds(2 * j + n, 1), :]
            decay = jnp.exp(jnp.where(keep, span, -1e30))
            decay_t = jnp.exp(jnp.where(keep_t, -span, -1e30))
            mix.append((scores * decay).astype(BF16))
            mix_t.append((scores_t * decay_t).astype(BF16))
            total_ds += ww[n * 128 : n * 128 + 128] * decay
        ds_acc[...] = total_ds
        yi[:, cols] = dot(jnp.concatenate(mix, axis=1), xx)
        dxi[:, cols] = dot(jnp.concatenate(mix_t, axis=1), gg)
        return carry

    lax.fori_loop(0, 8, pair, 0)

    for n, (d, t, source, target) in enumerate(others):
        remote(dmsg.at[0], dr.at[source], s0.at[d], r0.at[d], target).wait_recv()
        remote(msg.at[t], rmsg.at[source], s1.at[d], r1.at[d], target).wait_recv()
    state = jnp.zeros((64, 128), F32)
    for i in range(16):
        res[i, 0] = state.astype(BF16)
        state = jnp.exp(dr[i][0:1]) * state + rmsg[i, 0].astype(F32)
    state = jnp.zeros((64, 128), F32)
    for i in reversed(range(16)):
        res[i, 1] = state.astype(BF16)
        state = jnp.exp(dr[i][0:1]) * state + rmsg[i, 1].astype(F32)
    for d, t, source, target in others:
        copy = remote(res.at[t], rres.at[chip], s2.at[d], r2.at[d], target)
        copy.start()
        copies.append(copy)
    rres[pl.ds(chip, 1)] = res[pl.ds(chip, 1)]

    lax.fori_loop(8, 16, pair, 0)

    for d, t, source, target in others:
        remote(res.at[t], rres.at[source], s2.at[d], r2.at[d], target).wait_recv()
    for j in range(8):
        l = slice(j * 128, j * 128 + 128)
        at = pl.ds(c, 1)
        eo = jnp.exp(te[0, at, :, l][0][0:1])
        em = jnp.exp(te[1, at, :, l][0][0:1])
        own_f, own_b = stf[at, 0, :, l][0], stf[at, 1, :, l][0]
        mate_f, mate_b = pst[0, :, l].astype(F32), pst[1, :, l].astype(F32)
        start0 = jnp.concatenate([rres[2 * j, 0], rres[2 * j + 1, 0]], axis=0).astype(F32)
        end1 = jnp.concatenate([rres[2 * j, 1], rres[2 * j + 1, 1]], axis=0).astype(F32)
        start1 = jnp.where(first, eo, em) * start0 + jnp.where(first, own_f, mate_f)
        end0 = jnp.where(first, mate_b, own_b) + jnp.where(first, em, eo) * end1
        se[at, 0, :, l] = jnp.where(first, start0, start1).astype(BF16)[None]
        se[at, 1, :, l] = jnp.where(first, end0, end1).astype(BF16)[None]
        hs[0, :, l] = jnp.where(first, start1, start0).astype(BF16)
        hs[1, :, l] = jnp.where(first, end1, end0).astype(BF16)
    back = remote(hs, se.at[c], d_sem.at[4], d_sem.at[5], mate)
    back.start()
    ds = ds_acc[...]
    ds_t = ds.T.astype(BF16)
    ds = ds.astype(BF16)
    segment = jnp.where(
        lax.broadcasted_iota(jnp.int32, (2048, 128), 0) // 64 == lax.broadcasted_iota(jnp.int32, (2048, 128), 1), 1.0, 0.0
    ).astype(BF16)

    def by_head(values):
        high = values.astype(BF16)
        low = (values - high.astype(F32)).astype(BF16)
        part = segment[: values.shape[1]]
        return high, low

    grad_c = dot(ds, bm)
    grad_b = dot(ds_t, cm)
    back.wait_send()
    remote(hs, se.at[1 - c], d_sem.at[4], d_sem.at[5], mate).wait_recv()
    p1 = jnp.zeros((count, 128), F32)
    p2 = jnp.zeros((count, 128), F32)
    p3 = jnp.zeros((count, 128), F32)
    he = jnp.zeros((8, 128), F32)

    def heads(values, part):
        high = values.astype(BF16)
        low = (values - high.astype(F32)).astype(BF16)
        return dot(high, part) + dot(low, part)

    for q in range(4):
        half, l = q // 2, slice(q % 2 * 512, q % 2 * 512 + 512)
        cols = slice(q * 512, q * 512 + 512)
        part = segment[cols]
        st, en = se[half, 0, :, l], se[half, 1, :, l]
        xs = x_r[:, cols].astype(F32)
        gs = g_r[:, cols].astype(F32)
        skip = ske[0:1, cols]
        yo = yi[:, cols] + ece[:, cols] * dot(cm, st)
        dxs = tle[:, cols] * dot(bm, en)
        dxn = dxi[:, cols] + dxs
        y_o[:, cols] = (yo + skip * xs).astype(BF16)
        dx = (dte[:, cols] * dxn + skip * gs).astype(BF16)
        lo, hi = q * 512, q * 512 + 512
        if hi <= 1152:
            ga_o[:, lo:hi] = dx
        elif lo >= 1152:
            gb_o[:, lo - 1152 : hi - 1152] = dx
        else:
            ga_o[:, lo:1152] = dx[:, : 1152 - lo]
            gb_o[:, : hi - 1152] = dx[:, 1152 - lo :]
        p1 += heads(gs * yo, part)
        p2 += heads(xs * dxn, part)
        p3 += heads(xs * dxs, part)
        both = jnp.sum(st.astype(F32) * en.astype(F32), axis=0, keepdims=True)
        he += heads(jnp.broadcast_to(both, (8, 512)), part)
        grad_c += dot_nt(gec[:, cols], st)
        grad_b += dot_nt(xt[:, cols], en)
    last = jnp.sum(dt * p3, axis=0, keepdims=True) + jnp.exp(total) * he[0:1]
    dloga = dot(upper, p1 - dt * p2, lax.Precision.HIGHEST) + last
    draw = (p2 + decay_rate * dloga) * sig
    gb_o[:, 896:1024] = grad_b.astype(BF16)
    gb_o[:, 1024:1152] = grad_c.astype(BF16)
    gb_o[:, 1152:1184] = draw[:, :32].astype(BF16)
    for copy in copies:
        copy.wait_send()


def layer(x, bc, raw, a_log, dt_bias, d_skip, g):
    count, inner = x.shape
    sd = jax.ShapeDtypeStruct
    vm = pltpu.VMEM
    dma = pltpu.SemaphoreType.DMA
    return pl.pallas_call(
        scan_kernel,
        out_shape=(sd((count, inner), BF16), sd((count, 1152), BF16), sd((count, 1184), BF16)),
        in_specs=[VM] * 7,
        out_specs=(VM, VM, VM),
        scratch_shapes=[
            vm((count, inner), F32), vm((count, inner), F32), vm((count, inner), F32),
            vm((count, 2 * inner), F32), vm((128, count), F32),
            vm((count, inner), BF16), vm((count, inner), BF16), vm((count, inner), BF16),
            vm((count, inner), F32), vm((count, inner), F32), vm((128, 128), F32),
            vm((2, 2, 128, 1024), F32), vm((2, 128, 1024), BF16), vm((2, 128, 1024), BF16),
            vm((8, 128), F32), vm((8, 128), F32), vm((2, 2, 8, 1024), F32),
            vm((16, 2, 64, 128), BF16), vm((16, 2, 64, 128), BF16),
            vm((8, 8, 128), F32), vm((16, 8, 128), F32),
            vm((16, 2, 64, 128), BF16), vm((16, 2, 64, 128), BF16),
            vm((2, 2, 128, 1024), BF16), vm((2, 128, 1024), BF16), vm((8, inner), F32),
            dma((6,)), dma((16,)), dma((16,)), dma((16,)), dma((16,)), dma((16,)), dma((16,)),
        ],
        compiler_params=pltpu.CompilerParams(collective_id=1, has_side_effects=True, vmem_limit_bytes=LIMIT),
    )(x, bc, raw, a_log.reshape(1, -1), dt_bias.reshape(1, -1), d_skip.reshape(1, -1), g)


class Ring:
    def __init__(self, me, plus, minus, src, got, send, recv):
        self.me, self.plus, self.minus, self.src, self.got = me, plus, minus, src, got
        self.send, self.recv = send, recv
        self.h = src.shape[1] // 2
        self.copies = []

    def part(self, step, half):
        return self.src.at[(self.me + step) % 4, pl.ds(half * self.h, self.h)]

    def go(self, n, block, target):
        copy = remote(block, self.got.at[n], self.send.at[n], self.recv.at[n], target)
        copy.start()
        self.copies.append(copy)

    def far(self):
        self.go(0, self.part(2, 0), self.plus)
        self.go(1, self.part(2, 1), self.minus)

    def near(self, step):
        if step == 1:
            self.go(2, self.part(1, 1), self.plus)
        else:
            self.go(3, self.part(3, 0), self.minus)

    def landed(self, n):
        remote(self.part(0, 0), self.got.at[n], self.send.at[n], self.recv.at[n], self.plus).wait_recv()
        return self.got[n].astype(F32)

    def add(self, step, half, n):
        at = (self.me + step) % 4
        rows = slice(half * self.h, half * self.h + self.h)
        self.src[at, rows] = (self.src[at, rows].astype(F32) + self.landed(n)).astype(BF16)

    def middle(self):
        self.add(1, 0, 0)
        self.go(4, self.part(1, 0), self.plus)
        self.add(3, 1, 1)
        self.go(5, self.part(3, 1), self.minus)

    def end(self):
        low = self.src[self.me, : self.h].astype(F32) + self.landed(3)
        high = self.src[self.me, self.h :].astype(F32) + self.landed(2)
        return low + self.landed(4), high + self.landed(5)


def grad_kernel(
    ga, gb, wf, t1, t2, gt_o, gw_o,
    wbuf, a2, b2, p1, p2, g1, g2, q1, q2, h1, h2, z1, z2, y1, y2,
    w_sem, d_sem, s1, r1, s2, r2, s3, r3, s4, r4, s5, r5, s6, r6,
):
    xh, z, c, xl, y = place()
    x = xh * 2 + xl
    right, left = along_x((x + 1) % 4), along_x((x + 3) % 4)
    up, down = {"y": (y + 1) % 4}, {"y": (y + 3) % 4}
    mate = {"c": 1 - c}
    zs = [(d, (z + d) % 8, {"z": (z + d) % 8}) for d in range(1, 8)]
    load = pltpu.make_async_copy(wf, wbuf, w_sem)
    load.start()
    greet([mate, right, left, up, down] + [o[2] for o in zs])
    count = ga.shape[0]
    ca = remote(ga, a2.at[1], d_sem.at[0], d_sem.at[1], mate)
    cb = remote(gb, b2.at[1], d_sem.at[2], d_sem.at[3], mate)
    ca.start()
    cb.start()
    a2[0] = ga[...]
    b2[0] = gb[...]
    ring1 = Ring(x, right, left, p1, g1, s1, r1)
    ring2 = Ring(y, up, down, p2, g2, s2, r2)

    def partial(p, t, both, at):
        lhs = t[at].reshape(256, 2 * count)
        p[at] = (dot(lhs[:, :count], both[0]) + dot(lhs[:, count:], both[1])).astype(BF16)

    ca.wait()
    partial(p1, t1, a2, (x + 2) % 4)
    ring1.far()
    cb.wait()
    partial(p2, t2, b2, (y + 2) % 4)
    ring2.far()
    for step in (1, 3):
        partial(p1, t1, a2, (x + step) % 4)
        ring1.near(step)
        partial(p2, t2, b2, (y + step) % 4)
        ring2.near(step)
    partial(p1, t1, a2, x)
    partial(p2, t2, b2, y)

    load.wait()

    def tokens(k, carry):
        w = wbuf[k]
        cols = pl.ds(pl.multiple_of(k * 256, 256), 256)
        gt_o[:, cols] = (dot_nt(ga[...], w[:, :1152]) + dot_nt(gb[...], w[:, 1152:])).astype(BF16)
        return carry

    lax.fori_loop(0, 4, tokens, 0)
    ring1.middle()
    ring2.middle()
    lax.fori_loop(4, 8, tokens, 0)

    ring3 = Ring(y, up, down, q1, h1, s3, r3)
    ring4 = Ring(x, right, left, q2, h2, s4, r4)
    for ring, nxt, q in ((ring1, ring3, q1), (ring2, ring4, q2)):
        low, high = ring.end()
        for k in range(2):
            q[k] = low[k * 64 : k * 64 + 64].astype(BF16)
            q[k + 2] = high[k * 64 : k * 64 + 64].astype(BF16)
        nxt.far()
        nxt.near(1)
        nxt.near(3)
    ring3.middle()
    ring4.middle()
    copies = []
    for ring, zb, yb, s, r in ((ring3, z1, y1, s5, r5), (ring4, z2, y2, s6, r6)):
        low, high = ring.end()
        for k in range(4):
            zb[k] = low[k * 8 : k * 8 + 8].astype(BF16)
            zb[k + 4] = high[k * 8 : k * 8 + 8].astype(BF16)
        for d, t, target in zs:
            copy = remote(zb.at[t], yb.at[d], s.at[d], r.at[d], target)
            copy.start()
            copies.append(copy)
    for zb, yb, s, r, lo in ((z1, y1, s5, r5, 0), (z2, y2, s6, r6, 1152)):
        out = zb[z].astype(F32)
        for d, t, target in zs:
            remote(zb.at[t], yb.at[d], s.at[d], r.at[d], target).wait_recv()
            out += yb[d].astype(F32)
        gw_o[:, lo : lo + out.shape[1]] = out
    for ring in (ring1, ring2, ring3, ring4):
        for copy in ring.copies:
            copy.wait_send()
    for copy in copies:
        copy.wait_send()


def weight_grads(ga, gb, wf, t1, t2):
    count = ga.shape[0]
    wa, wb = ga.shape[1], gb.shape[1]
    sd = jax.ShapeDtypeStruct
    vm = pltpu.VMEM
    dma = pltpu.SemaphoreType.DMA
    return pl.pallas_call(
        grad_kernel,
        out_shape=(sd((count, 2048), BF16), sd((8, wa + wb), F32)),
        in_specs=[VM, VM, ANY, VM, VM],
        out_specs=(VM, VM),
        scratch_shapes=[
            vm(wf.shape, BF16),
            vm((2, count, wa), BF16), vm((2, count, wb), BF16),
            vm((4, 256, wa), BF16), vm((4, 256, wb), BF16),
            vm((6, 128, wa), BF16), vm((6, 128, wb), BF16),
            vm((4, 64, wa), BF16), vm((4, 64, wb), BF16),
            vm((6, 32, wa), BF16), vm((6, 32, wb), BF16),
            vm((8, 8, wa), BF16), vm((8, 8, wb), BF16),
            vm((8, 8, wa), BF16), vm((8, 8, wb), BF16),
            dma, dma((4,)),
        ]
        + [dma((6,))] * 8
        + [dma((8,))] * 4,
        compiler_params=pltpu.CompilerParams(collective_id=2, has_side_effects=True, vmem_limit_bytes=LIMIT),
    )(ga, gb, wf, t1, t2)


def per_device(tokens, w_in, a_log, dt_bias, d_skip, grad_y):
    count, width = tokens.shape[1:]
    inner = grad_y.shape[2]
    x, bc, raw, wf, t1, t2 = gather(tokens.reshape(count, width), w_in)
    y, ga, gb = layer(x, bc, raw, a_log, dt_bias, d_skip, grad_y.reshape(count, inner))
    gt, gw = weight_grads(ga, gb, wf, t1, t2)
    return (y.reshape(1, count, inner), gt.reshape(1, count, width), gw)


def solution(mesh):
    torus = Mesh(mesh.devices.reshape(2, 8, 2, 2, 4), ("xh", "z", "c", "xl", "y"))
    placed = (P(ZERO, SEQ, None), P(ZERO, None), P(), P(), P(), P(ZERO, SEQ, None))
    return jax.shard_map(
        per_device,
        mesh=torus,
        in_specs=placed,
        out_specs=(P(ZERO, SEQ, None), P(ZERO, SEQ, None), P(SEQ + ZERO, None)),
        check_vma=False,
    )
```

time: 612 us -> 142 us (0.23)
  waiting for transfers between devices: 478 us -> 0 us
  Pallas kernels: 0 us -> 137 us
  blocking collectives: 39.3 us -> 0 us
  other arithmetic: 30.6 us -> 0 us
  matrix products: 28.6 us -> 0 us
  between operations: 14.7 us -> 0.69 us
  starting transfers between devices: 13.3 us -> 0 us
    all_gather x8 -> x0, waiting for transfers between devices: 428 us -> none  [the longest x6 266 us: prefix_by_axis(): pieces = jax.tree.map(lambda part: lax.all_gather(part, axis), so_far)]
    pallas_call x0 -> x3, Pallas kernels: none -> 137 us  [the longest x1 49.7 us: layer(): pl.pallas_call(scan_kernel, out_shape=(sd((count, inner), BF16), sd((coun...]
    all_to_all x1 -> x0, waiting for transfers between devices: 48.9 us -> none  [summed_on_arrival(): blocks = lax.all_to_all(cut_along(array, dim, size), axis, 0, 0, tiled=True)]
    dot_general x16 -> x0, matrix products: 28.6 us -> none  [the longest x1 6.12 us: per_device(): lax.dot_general(gproj, full_w, (((1,), (1,)), ((), ())), preferred_elemen...]
    all_gather x4 -> x0, blocking collectives: 27 us -> none  [prefix_by_axis(): pieces = jax.tree.map(lambda part: lax.all_gather(part, axis), so_far)]
    add x4 -> x0, other arithmetic: 14.8 us -> none  [the longest x2 7.47 us: carry_backward(): later[1] + jnp.exp(later[0])[:, None, None] * earlier[1]]
    all_to_all x1 -> x0, starting transfers between devices: 13 us -> none  [summed_on_arrival(): blocks = lax.all_to_all(cut_along(array, dim, size), axis, 0, 0, tiled=True)]
    reduce_sum x4 -> x0, other arithmetic: 12.5 us -> none  [the longest x1 10.4 us: block_ssd(): jnp.exp(cum[-1])[:, None, None] * start]
  transfers between devices with their start and end apart: 9 -> 0, of which waited for: 9 -> 0; matrix products, arithmetic and copies ran while one was open for 5% -> 0% of each run, Pallas kernels for 0% -> 0%
where the time goes in v1:
time: 142 us
  Pallas kernels  137 us (96%)
  local copies, waits for them, and re-layouts  5.04 us (4%)
    pallas_call x1, Pallas kernels, layer(): pl.pallas_call(scan_kernel, out_shape=(sd((count, inner), BF16), sd((coun...  49.7 us
    pallas_call x1, Pallas kernels, weight_grads(): pl.pallas_call(grad_kernel, out_shape=(sd((count, 2048), BF16), sd((8, wa...  46 us
    pallas_call x1, Pallas kernels, gather(): pl.pallas_call(gather_kernel, out_shape=(sd((count, 2048), BF16), sd((cou...  40.8 us
    unnamed x10, local copies, waits for them, and re-layouts  5.04 us

profile of v1, /device:TPU:1, one launch (start us, length us, event | category | flops | bytes accessed | tf_op | source)
XLA Modules:
  0.0 142.3 jit_solution(8170217206611309743)
XLA Ops:
  0.6 2.4 %copy.9.w = bf16[256,2336]{1,0:T(8,128)(2,1)} copy(bf16[256,2336]{0,1:T(8,128)(2,1)} %param.7) | data formatting | bytes 2392064 | tf_op args[1]
  3.0 40.8 %shard_map.85 = (bf16[128,2048]{1,0:T(8,128)(2,1)}, bf16[128,256]{1,0:T(8,128)(2,1)}, f32[128,32]{1,0:T(8,128)}, bf16[8,256,2336]{2,1,0:T(8,128)(2,1)}, bf16[4,4...) custom-call(bf16[128,2048]{1,0:T(8,128)(2,1)} %bitcast.7, bf16[256,2336]{1,0:T(8,128)(2,1)} %copy.9.w), custom_call_target="tpu_custom_call" | custom-call | tf_op jit(solution)/shard_map/pallas_call | solution.py:197
  43.8 49.7 %shard_map.86 = (bf16[128,2048]{1,0:T(8,128)(2,1)}, bf16[128,1152]{1,0:T(8,128)(2,1)}, bf16[128,1184]{1,0:T(8,128)(2,1)}) custom-call(bf16[128,2048]{1,0:T(8,128)(2,1)} %get-tuple-element.14.x_r, bf16[128,256]{1,0:T(8,128)(2,1)} %get-tuple-element.15.bc_r, f32[128,32]{1,0:T(8,128)} %get-tuple-element.16.raw_r, f32[1,32]{1,0:T(1,128)} %bitcast.11, ...), custom_call_target="tpu_custom_call" | custom-call | tf_op jit(solution)/shard_map/pallas_call | solution.py:473
  93.6 0.0 copy-start
  93.6 46.0 %shard_map.87 = (bf16[128,2048]{1,0:T(8,128)(2,1)}, f32[8,2336]{1,0:T(8,128)}) custom-call(bf16[128,1152]{1,0:T(8,128)(2,1)} %get-tuple-element.18.ga, bf16[128,1184]{1,0:T(8,128)(2,1)} %get-tuple-element.19.gb, bf16[8,256,2336]{2,1,0:T(8,128)(2,1)} %get-tuple-element.20.wf, bf16[4,4,64,256]{3,2,1,0:T(8,128)(2,1)} %get-tuple-element.21.t1, ...), custom_call_target="tpu_custom_call" | custom-call | tf_op jit(solution)/shard_map/pallas_call | solution.py:637
  139.6 0.0 copy-start.1
  139.6 0.0 copy-start.2
  139.6 0.0 copy-done
  139.6 0.8 copy.13
  140.4 0.4 copy-done.1
  140.8 0.8 copy.14
  141.6 0.0 copy-done.2
  141.6 0.6 copy.15
Async XLA Ops:
  93.6 46.1 %copy-start = (bf16[128,2048]{1,0:T(8,128)(2,1)S(1)}, bf16[128,2048]{1,0:T(8,128)(2,1)}, u32[]{:S(2)}) copy-start(bf16[128,2048]{1,0:T(8,128)(2,1)} %get-tuple-element.17) | copy-start | bytes 1572868
  139.6 1.2 copy-start.1
  139.6 2.0 %copy-start.2 = (f32[8,2336]{1,0:T(8,128)S(1)}, f32[8,2336]{1,0:T(8,128)}, u32[]{:S(2)}) copy-start(f32[8,2336]{1,0:T(8,128)} %get-tuple-element.30) | copy-start | bytes 224260

commit v2 on v0

v2 whole, which is shorter than its diff:
```python
import jax
import jax.numpy as jnp
from jax import lax
from jax.experimental import pallas as pl
from jax.experimental.pallas import tpu as pltpu
from jax.sharding import Mesh
from jax.sharding import PartitionSpec as P

SEQ = ("xh", "z", "c")
ZERO = ("xl", "y")
MESH = pl.DeviceIdType.MESH
F32 = jnp.float32
BF16 = jnp.bfloat16
LIMIT = 62 * 1024 * 1024
VM = pl.BlockSpec(memory_space=pltpu.VMEM)
ANY = pl.BlockSpec(memory_space=pl.ANY)
INNER = 2048
EDGE_SMALL, EDGE_LARGE = 384, 400
WX, WZ, WY = 768, 768, 800


def remote(src, dst, send, recv, target):
    return pltpu.make_async_remote_copy(
        src_ref=src, dst_ref=dst, send_sem=send, recv_sem=recv, device_id=target, device_id_type=MESH
    )


def along_x(x):
    return {"xh": x // 2, "xl": x % 2}


def dot(a, b, precision=None):
    return jnp.dot(a, b, preferred_element_type=F32, precision=precision)


def dot_nt(a, b):
    return lax.dot_general(a, b, (((1,), (1,)), ((), ())), preferred_element_type=F32)


class Place:
    def __init__(self):
        self.xh, self.z, self.c, self.xl, self.y = (lax.axis_index(a) for a in ("xh", "z", "c", "xl", "y"))
        self.x = self.xh * 2 + self.xl
        self.chip = self.xh * 8 + self.z
        self.right, self.left = along_x((self.x + 1) % 4), along_x((self.x + 3) % 4)
        self.up, self.down = {"y": (self.y + 1) % 4}, {"y": (self.y + 3) % 4}
        self.fore, self.aft = {"z": (self.z + 1) % 8}, {"z": (self.z + 7) % 8}
        self.mate = {"c": 1 - self.c}
        self.others = []
        for d in range(1, 16):
            t = (self.chip + d) % 16
            self.others.append((d, t, (self.chip + 16 - d) % 16, {"xh": t // 8, "z": t % 8}))

    def greet(self):
        barrier = pltpu.get_barrier_semaphore()
        targets = [self.mate, self.right, self.left, self.up, self.down] + [o[3] for o in self.others]
        for target in targets:
            pl.semaphore_signal(barrier, inc=1, device_id=target, device_id_type=MESH)
        pl.semaphore_wait(barrier, len(targets))


class Gather:
    def __init__(self, at, w, wbuf, s):
        self.at, self.w, self.wbuf, self.s = at, w, wbuf, s
        self.sends, self.n = [], 0
        self.rel = [self.shard(0, 3), self.shard(0, 1), self.shard(0, 2)] + [self.shard(1, d) for d in (0, 3, 1, 2)]
        self.mine = self.shard(0, 0)

    def shard(self, flip, dy):
        return (self.at.xl + flip) % 2 * 4 + (self.at.y + dy) % 4

    def rows(self, part, core=None):
        core = self.at.c if core is None else core
        odd = self.at.z % 2
        base = core * (2 * EDGE_SMALL + EDGE_LARGE)
        far = EDGE_SMALL + EDGE_LARGE
        if part == "a":
            start, size = base + odd * far, EDGE_SMALL
        elif part == "b":
            start, size = base + EDGE_SMALL, EDGE_LARGE
        elif part in ("a0", "a1"):
            start, size = base + odd * far + (part == "a1") * (EDGE_SMALL // 2), EDGE_SMALL // 2
        else:
            start, size = base + (1 - odd) * far + (part == "m1") * (EDGE_SMALL // 2), EDGE_SMALL // 2
        return pl.ds(pl.multiple_of(start, 16), size)

    def block(self, k, part, core=None):
        return self.wbuf.at[k, self.rows(part, core)]

    def send(self, k, part, to, slot, lane):
        block = self.block(k, part)
        copy = remote(block, block, self.s["send"].at[self.n], self.s["ici"].at[slot, lane], to)
        self.n += 1
        copy.start()
        self.sends.append(copy)

    def depth_send(self, k, slot):
        self.send(k, "a0", self.at.fore, slot, 2)
        self.send(k, "a1", self.at.aft, slot, 3)

    def begin(self):
        at = self.at
        self.send(self.mine, "a", at.up, 0, 0)
        self.send(self.mine, "b", at.down, 1, 1)
        self.send(self.mine, "a", at.left, 3, 0)
        self.send(self.mine, "b", at.right, 3, 1)
        self.send(self.mine, "b", at.up, 0, 1)
        self.send(self.mine, "a", at.down, 1, 0)

    def arrive(self, slot, lane):
        part = ("a", "b", "m0", "m1")[lane]
        block = self.block(self.rel[slot], part)
        remote(block, block, self.s["send"].at[0], self.s["ici"].at[slot, lane], self.at.mate).wait_recv()
        copy = remote(block, block, self.s["d2d_send"].at[slot, lane], self.s["d2d"].at[slot, lane], self.at.mate)
        copy.start()
        self.sends.append(copy)

    def a(self, slot, *onward):
        self.arrive(slot, 0)
        for to, there in onward:
            self.send(self.rel[slot], "a", to, there, 0)
        self.depth_send(self.rel[slot], slot)

    def b(self, slot, *onward):
        self.arrive(slot, 1)
        for to, there in onward:
            self.send(self.rel[slot], "b", to, there, 1)

    def m(self, slot):
        self.arrive(slot, 2)
        self.arrive(slot, 3)

    def whole(self, slot):
        for lane, part in enumerate(("a", "b", "m0", "m1")):
            block = self.block(self.rel[slot], part, 1 - self.at.c)
            remote(block, block, self.s["d2d_send"].at[slot, lane], self.s["d2d"].at[slot, lane], self.at.mate).wait_recv()


def spread(row):
    lane = lax.broadcasted_iota(jnp.int32, (row.shape[0], 128), 1)
    out = []
    for j in range(16):
        out.append(jnp.where(lane < 64, row[:, 2 * j : 2 * j + 1], row[:, 2 * j + 1 : 2 * j + 2]))
    return out


def heads(values, part):
    high = values.astype(BF16)
    low = (values - high.astype(F32)).astype(BF16)
    return dot(high, part) + dot(low, part)


class Ring4:
    def __init__(self, me, plus, minus, src, got, send, recv):
        self.me, self.plus, self.minus, self.src, self.got = me, plus, minus, src, got
        self.sem, self.recv = send, recv
        self.h = src.shape[1] // 2
        self.copies = []

    def part(self, step, half):
        return self.src.at[(self.me + step) % 4, pl.ds(half * self.h, self.h)]

    def go(self, n, block, target):
        copy = remote(block, self.got.at[n], self.sem.at[n], self.recv.at[n], target)
        copy.start()
        self.copies.append(copy)

    def far(self):
        self.go(0, self.part(2, 0), self.plus)
        self.go(1, self.part(2, 1), self.minus)

    def near(self, step):
        if step == 1:
            self.go(2, self.part(1, 1), self.plus)
        else:
            self.go(3, self.part(3, 0), self.minus)

    def landed(self, n):
        remote(self.part(0, 0), self.got.at[n], self.sem.at[n], self.recv.at[n], self.plus).wait_recv()
        return self.got[n].astype(F32)

    def add(self, step, half, n):
        at = (self.me + step) % 4
        rows = slice(half * self.h, half * self.h + self.h)
        self.src[at, rows] = (self.src[at, rows].astype(F32) + self.landed(n)).astype(BF16)

    def middle(self):
        self.add(1, 0, 0)
        self.go(4, self.part(1, 0), self.plus)
        self.add(3, 1, 1)
        self.go(5, self.part(3, 1), self.minus)

    def end(self):
        low = self.src[self.me, : self.h].astype(F32) + self.landed(3)
        high = self.src[self.me, self.h :].astype(F32) + self.landed(2)
        return low + self.landed(4), high + self.landed(5)


class Ring8:
    def __init__(self, me, plus, minus, src, got, send, recv):
        self.me, self.src, self.got, self.sem, self.recv = me, src, got, send, recv
        self.to = (plus, minus)
        self.h = src.shape[1] // 2
        self.copies = []

    def piece(self, way, s):
        return (self.me + (s if way == 0 else 8 - s)) % 8

    def slot(self, way, half, s):
        return (way * 2 + half) * 4 + s

    def go(self, way, half, s):
        block = self.src.at[self.piece(way, s), pl.ds(half * self.h, self.h)]
        n = self.slot(way, half, s - 1)
        copy = remote(block, self.got.at[n], self.sem.at[n], self.recv.at[n], self.to[way])
        copy.start()
        self.copies.append(copy)

    def landed(self, way, half, s):
        n = self.slot(way, half, s)
        block = self.src.at[self.me, pl.ds(0, self.h)]
        remote(block, self.got.at[n], self.sem.at[n], self.recv.at[n], self.to[way]).wait_recv()
        return self.got[n].astype(F32)

    def on(self, way, half, s):
        at = self.piece(way, s)
        rows = slice(half * self.h, half * self.h + self.h)
        self.src[at, rows] = (self.src[at, rows].astype(F32) + self.landed(way, half, s)).astype(BF16)
        self.go(way, half, s)

    def far(self):
        self.go(0, 0, 4)
        self.go(1, 1, 4)

    def next_far(self, way):
        self.go(way, 1 - way, 3)

    def long(self, s):
        self.on(0, 0, s)
        self.on(1, 1, s)

    def short(self, s):
        self.on(0, 1, s)
        self.on(1, 0, s)

    def end(self):
        low = self.src[self.me, : self.h].astype(F32) + self.landed(1, 0, 0)
        high = self.src[self.me, self.h :].astype(F32) + self.landed(0, 1, 0)
        return low + self.landed(0, 0, 0), high + self.landed(1, 1, 0)


def kernel(names, *refs):
    r = dict(zip(names, refs))
    at = Place()
    c, x, y, z, chip, mate = at.c, at.x, at.y, at.z, at.chip, at.mate
    first = c == 0
    own = pl.ds(c, 1)

    tok, acc, wbuf = r["tok"], r["acc"], r["wbuf"]
    count = tok.shape[0]
    depth = wbuf.shape[2]
    gather = Gather(at, r["w"], wbuf, {"send": r["g_send"], "ici": r["g_ici"], "d2d_send": r["g_d2d_send"], "d2d": r["g_d2d"]})
    w_copy = pltpu.make_async_copy(r["w"], wbuf.at[gather.mine], r["in_sem"].at[0])
    tok_copy = pltpu.make_async_copy(r["tokens"], tok, r["in_sem"].at[1])
    g_copy = pltpu.make_async_copy(r["grad_y"], r["g"], r["in_sem"].at[2])
    w_copy.start()
    tok_copy.start()
    g_copy.start()
    at.greet()
    w_copy.wait()
    gather.begin()
    tok_copy.wait()
    tt, tt3 = r["tt"], r["tt3"]
    for i in range(16):
        block = tok[:, i * 128 : (i + 1) * 128].astype(F32).T
        for n in range(16):
            core, xlow, yy = n // 8, n // 4 % 2, n % 4
            rows = block[n * 8 : n * 8 + 8, :]
            xx, zz = i // 8 * 2 + xlow, i % 8
            tt[core, xx, yy, zz * 8 : zz * 8 + 8, :] = rows
            tt3[core, zz, xx * 32 + yy * 8 : xx * 32 + yy * 8 + 8, :] = rows
    tb, tb3, tr, tr3 = r["tb"], r["tb3"], r["tr"], r["tr3"]
    tb[...] = tt[...].astype(BF16)
    tb3[...] = tt3[...].astype(BF16)
    swap = remote(tb.at[1 - c], tr, r["tok_sem"].at[0], r["tok_sem"].at[1], mate)
    swap3 = remote(tb3.at[1 - c], tr3, r["tok_sem"].at[2], r["tok_sem"].at[3], mate)
    swap.start()
    swap3.start()
    t1, t2, t3 = r["t1"], r["t2"], r["t3"]

    def place_rows(lo, one, three):
        t1[:, :, :, lo : lo + 128] = one
        t3[:, :, lo : lo + 128] = three
        for i in range(4):
            for j in range(4):
                t2[j, i, :, lo : lo + 128] = one[i, j]

    place_rows(0, tb[own][0], tb3[own][0])
    acc[...] = jnp.zeros_like(acc)

    def multiply(*ks):
        def body(i, carry):
            k = ks[0]
            for n in range(1, len(ks)):
                k = jnp.where(i == n, ks[n], k)
            acc[...] += dot_nt(tok[:, pl.ds(pl.multiple_of(k * depth, depth), depth)], wbuf[k])
            return carry

        lax.fori_loop(0, len(ks), body, 0)

    ga, gb, gm, rel = gather.a, gather.b, gather.m, gather.rel
    with jax.named_scope("g1"):
        ga(0, (at.up, 2), (at.left, 4))
        gb(1, (at.down, 2), (at.right, 5))
        ga(3)
        gb(3)
    with jax.named_scope("g2"):
        gb(0, (at.right, 4))
        ga(1, (at.left, 5))
        ga(4)
        gb(5)
        gm(0)
        gm(3)
    with jax.named_scope("g3"):
        ga(2, (at.left, 6))
        gb(2, (at.right, 6))
        gb(4)
        ga(5)
        gather.whole(0)
        gather.whole(3)
        multiply(gather.mine, rel[0], rel[3])
    with jax.named_scope("g4"):
        gm(1)
        gm(4)
        ga(6)
        gb(6)
        gm(2)
        gm(5)
        for slot in (1, 4, 2, 5):
            gather.whole(slot)
    with jax.named_scope("g5"):
        multiply(rel[1], rel[4], rel[2], rel[5])
    with jax.named_scope("g6"):
        swap.wait()
        swap3.wait()
        place_rows(128, tr[...], tr3[...])
        gm(6)
        gather.whole(6)
    with jax.named_scope("g7"):
        multiply(rel[6])

    x_r, g_r = r["x"], r["g"]
    dte, ece, tle, cume, cumt = r["dte"], r["ece"], r["tle"], r["cume"], r["cumt"]
    xdt, xt, gec, yi, dxi, ds_acc = r["xdt"], r["xt"], r["gec"], r["yi"], r["dxi"], r["ds_acc"]
    stf, sst, pst, te, ske = r["stf"], r["sst"], r["pst"], r["te"], r["ske"]
    tot_s, tot_r, dmsg, dr = r["tot_s"], r["tot_r"], r["dmsg"], r["dr"]
    msg, rmsg, res, rres, se, hs = r["msg"], r["rmsg"], r["res"], r["rres"], r["se"], r["hs"]
    d_sem = r["d_sem"]
    copies = []
    with jax.named_scope("prep"):
        x_r[...] = acc[:, :INNER].astype(BF16)
        bm = acc[:, INNER : INNER + 128].astype(BF16)
        cm = acc[:, INNER + 128 : INNER + 256].astype(BF16)
        rowz = jnp.zeros((1, 96), F32)
        decay_rate = jnp.concatenate([-jnp.exp(r["a_log"][...]), rowz], axis=1)
        bias = jnp.concatenate([r["dt_bias"][...], rowz], axis=1)
        u = jnp.concatenate([acc[:, INNER + 256 :], jnp.zeros((count, 96), F32)], axis=1) + bias
        small = jnp.exp(-jnp.abs(u))
        dt = jnp.maximum(u, 0.0) + jnp.log1p(small)
        sig = jnp.where(u >= 0, 1.0, small) / (1.0 + small)
        ti = lax.broadcasted_iota(jnp.int32, (128, 128), 0)
        si = lax.broadcasted_iota(jnp.int32, (128, 128), 1)
        keep, keep_t = ti >= si, ti <= si
        lower = jnp.where(keep, 1.0, 0.0).astype(F32)
        upper = jnp.where(keep_t, 1.0, 0.0).astype(F32)
        cum = dot(lower, decay_rate * dt, lax.Precision.HIGHEST)
        total = cum[127:128, :]
        tot_s[...] = jnp.broadcast_to(total, (8, 128))
        tot_copy = remote(tot_s, tot_r, d_sem.at[0], d_sem.at[1], mate)
        tot_copy.start()
        growth = jnp.exp(cum)
        tail = jnp.exp(total - cum)
        cumt[...] = cum.T
        lane = lax.broadcasted_iota(jnp.int32, (count, 128), 1)
        for arr, dst in ((dt, dte), (tail, tle), (growth, ece)):
            for j, e in enumerate(spread(arr)):
                dst[:, j * 128 : (j + 1) * 128] = e
        xd = x_r[...].astype(F32) * dte[...]
        xdt[...] = xd.astype(BF16)
        xt[...] = (xd * tle[...]).astype(BF16)
        bt = bm.astype(F32).T.astype(BF16)
        ct = cm.astype(F32).T.astype(BF16)

    def local_states(kind, lhs, rhs):
        for half in range(2):
            stf[kind, half] = dot(lhs, rhs[:, half * 1024 : half * 1024 + 1024])
        sst[kind] = stf[kind, pl.ds(1 - c, 1)][0].astype(BF16)
        copy = remote(sst.at[kind], pst.at[kind], d_sem.at[2 + 2 * kind], d_sem.at[3 + 2 * kind], mate)
        copy.start()
        return copy

    with jax.named_scope("states"):
        st_copies = [local_states(0, bt, xt)]
        g_copy.wait()
        gec[...] = (g_r[...].astype(F32) * ece[...]).astype(BF16)
        st_copies.append(local_states(1, ct, gec))
        tot_copy.wait()
        for n, arr in enumerate((tot_s, tot_r)):
            for j, e in enumerate(spread(arr[...])):
                te[n, j // 8, :, j % 8 * 128 : j % 8 * 128 + 128] = e
        for j in range(8):
            l = slice(j * 128, j * 128 + 128)
            dmsg[j] = te[0, own, :, l][0] + te[1, own, :, l][0]
        dr[pl.ds(chip, 1)] = dmsg[pl.ds(chip // 2, 1)]
        for d, t, source, target in at.others:
            copy = remote(dmsg.at[t // 2], dr.at[chip], r["s0"].at[d], r["r0"].at[d], target)
            copy.start()
            copies.append(copy)
        e_own, e_mate = jnp.exp(te[0, own][0][0:1]), jnp.exp(te[1, own][0][0:1])
        e0 = jnp.where(first, e_own, e_mate)
        e1 = jnp.where(first, e_mate, e_own)

    def send_states(kind):
        st_copies[kind].wait()
        mine, theirs = stf[kind, own][0], pst[kind].astype(F32)
        early = jnp.where(first, mine, theirs)
        late = jnp.where(first, theirs, mine)
        whole = (e1 * early + late if kind == 0 else early + e0 * late).astype(BF16)
        for i in range(16):
            msg[kind, i] = whole[i % 2 * 64 : i % 2 * 64 + 64, i // 2 * 128 : i // 2 * 128 + 128]
        for d, t, source, target in at.others:
            copy = remote(msg.at[kind, t], rmsg.at[kind, chip], r["s1"].at[kind, d], r["r1"].at[kind, d], target)
            copy.start()
            copies.append(copy)
        rmsg[kind, pl.ds(chip, 1)] = msg[kind, pl.ds(chip, 1)]

    def scan_states(kind):
        for d, t, source, target in at.others:
            if kind == 0:
                remote(dmsg.at[0], dr.at[source], r["s0"].at[d], r["r0"].at[d], target).wait_recv()
            remote(msg.at[kind, t], rmsg.at[kind, source], r["s1"].at[kind, d], r["r1"].at[kind, d], target).wait_recv()
        state = jnp.zeros((64, 128), F32)
        for i in range(16) if kind == 0 else reversed(range(16)):
            res[kind, i] = state.astype(BF16)
            state = jnp.exp(dr[i][0:1]) * state + rmsg[kind, i].astype(F32)
        for d, t, source, target in at.others:
            copy = remote(res.at[kind, t], rres.at[kind, chip], r["s2"].at[kind, d], r["r2"].at[kind, d], target)
            copy.start()
            copies.append(copy)
        rres[kind, pl.ds(chip, 1)] = res[kind, pl.ds(chip, 1)]

    def take_states(kind):
        for d, t, source, target in at.others:
            remote(res.at[kind, t], rres.at[kind, source], r["s2"].at[kind, d], r["r2"].at[kind, d], target).wait_recv()
        for j in range(8):
            l = slice(j * 128, j * 128 + 128)
            got = jnp.concatenate([rres[kind, 2 * j], rres[kind, 2 * j + 1]], axis=0).astype(F32)
            mine, theirs = stf[kind, own, :, l][0], pst[kind, :, l].astype(F32)
            if kind == 0:
                edge, inside = got, e0[:, l] * got + jnp.where(first, mine, theirs)
                low, high = edge, inside
            else:
                edge, inside = got, jnp.where(first, theirs, mine) + e1[:, l] * got
                low, high = inside, edge
            se[kind, own, :, l] = jnp.where(first, low, high).astype(BF16)[None]
            hs[kind, :, l] = jnp.where(first, high, low).astype(BF16)
        copy = remote(hs.at[kind], se.at[kind, c], d_sem.at[6 + 2 * kind], d_sem.at[7 + 2 * kind], mate)
        copy.start()
        copies.append(copy)

    def mate_states(kind):
        remote(hs.at[kind], se.at[kind, 1 - c], d_sem.at[6 + 2 * kind], d_sem.at[7 + 2 * kind], mate).wait_recv()

    with jax.named_scope("send_f"):
        send_states(0)
    with jax.named_scope("send_b"):
        send_states(1)

    with jax.named_scope("pairs_prep"):
        scores = dot_nt(cm, bm)
        scores_t = dot_nt(bm, cm)
        ds_acc[...] = jnp.zeros_like(ds_acc)
        for j, e in enumerate(spread(jnp.broadcast_to(jnp.concatenate([r["d_skip"][...], rowz], axis=1), (8, 128)))):
            ske[:, j * 128 : (j + 1) * 128] = e
        for h in range(32):
            cume[:, h * 128 : h * 128 + 128] = jnp.broadcast_to(cum[:, h : h + 1], (count, 128))

    def pair(j, carry):
        cols = pl.ds(pl.multiple_of(j * 128, 128), 128)
        xj = xdt[:, cols]
        gj = g_r[:, cols]
        none = jnp.zeros_like(xj)
        xx = jnp.concatenate([jnp.where(lane < 64, xj, none), jnp.where(lane < 64, none, xj)], axis=0)
        gg = jnp.concatenate([jnp.where(lane < 64, gj, none), jnp.where(lane < 64, none, gj)], axis=0)
        ww = dot_nt(gg, xj)
        mix, mix_t = [], []
        total_ds = ds_acc[...]
        for n in range(2):
            span = cume[:, pl.ds(pl.multiple_of(j * 256 + n * 128, 128), 128)] - cumt[pl.ds(2 * j + n, 1), :]
            decay = jnp.exp(jnp.where(keep, span, -1e30))
            decay_t = jnp.exp(jnp.where(keep_t, -span, -1e30))
            mix.append((scores * decay).astype(BF16))
            mix_t.append((scores_t * decay_t).astype(BF16))
            total_ds += ww[n * 128 : n * 128 + 128] * decay
        ds_acc[...] = total_ds
        yi[:, cols] = dot(jnp.concatenate(mix, axis=1), xx)
        dxi[:, cols] = dot(jnp.concatenate(mix_t, axis=1), gg)
        return carry

    with jax.named_scope("pairs1"):
        lax.fori_loop(0, 6, pair, 0)
    with jax.named_scope("scan_f"):
        scan_states(0)
    with jax.named_scope("pairs2"):
        lax.fori_loop(6, 11, pair, 0)
    with jax.named_scope("scan_b"):
        scan_states(1)
    with jax.named_scope("pairs3"):
        lax.fori_loop(11, 16, pair, 0)
        ds = ds_acc[...]
        ds_t = ds.T.astype(BF16)
        ds = ds.astype(BF16)
        grad_c = dot(ds, bm)
        grad_b = dot(ds_t, cm)
    with jax.named_scope("take_f"):
        take_states(0)
        mate_states(0)
    segment = jnp.where(
        lax.broadcasted_iota(jnp.int32, (512, 128), 0) // 64 == lax.broadcasted_iota(jnp.int32, (512, 128), 1), 1.0, 0.0
    ).astype(BF16)
    y_v = r["y_v"]

    def place_heads(arrs):
        lane8 = lax.broadcasted_iota(jnp.int32, arrs[0].shape, 1)
        out = arrs[0]
        for q in range(1, 4):
            out = jnp.where(lane8 < 8 * q, out, pltpu.roll(arrs[q], 8 * q, 1))
        return out

    with jax.named_scope("y_part"):
        p1 = []
        for q in range(4):
            half, l = q // 2, slice(q % 2 * 512, q % 2 * 512 + 512)
            cols = slice(q * 512, q * 512 + 512)
            st = se[0, half, :, l]
            xs = x_r[:, cols].astype(F32)
            yo = yi[:, cols] + ece[:, cols] * dot(cm, st)
            y_v[:, cols] = (yo + ske[0:1, cols] * xs).astype(BF16)
            p1.append(heads(g_r[:, cols].astype(F32) * yo, segment))
            grad_c += dot_nt(gec[:, cols], st)
        p1 = place_heads(p1)
        y_copy = pltpu.make_async_copy(y_v, r["y_out"], r["in_sem"].at[0])
        y_copy.start()
    with jax.named_scope("take_b"):
        take_states(1)
        mate_states(1)

    gx, gz, gy = r["gx"], r["gz"], r["gy"]
    swaps = {}

    def swap_grads(n, buf):
        copy = remote(buf.at[0], buf.at[1], r["gs_sem"].at[n], r["gr_sem"].at[n], mate)
        copy.start()
        swaps[n] = copy

    p2, p3, he = [], [], []

    def x_part(q):
        half, l = q // 2, slice(q % 2 * 512, q % 2 * 512 + 512)
        cols = slice(q * 512, q * 512 + 512)
        en = se[1, half, :, l]
        xs = x_r[:, cols].astype(F32)
        dxs = tle[:, cols] * dot(bm, en)
        dxn = dxi[:, cols] + dxs
        dx = (dte[:, cols] * dxn + ske[0:1, cols] * g_r[:, cols].astype(F32)).astype(BF16)
        if q == 0:
            gx[0, :, :512] = dx
        elif q == 1:
            gx[0, :, 512:] = dx[:, :256]
            gz[0, :, :256] = dx[:, 256:]
        elif q == 2:
            gz[0, :, 256:] = dx
        else:
            gy[0, :, :512] = dx
        p2.append(heads(xs * dxn, segment))
        p3.append(heads(xs * dxs, segment))
        both = jnp.sum(se[0, half, :, l].astype(F32) * en.astype(F32), axis=0, keepdims=True)
        he.append(heads(jnp.broadcast_to(both, (8, 512)), segment))
        return dot_nt(xt[:, cols], en)

    ring_x = Ring4(x, at.right, at.left, r["px"], r["got_x"], r["sx"], r["rx"])
    ring_y = Ring4(y, at.up, at.down, r["py"], r["got_y"], r["sy"], r["ry"])
    ring_z = Ring8(z, at.fore, at.aft, r["pz"], r["got_z"], r["sz"], r["rz"])

    def partial(p, lhs, both, piece):
        rows = p.shape[1]
        lhs = lhs[piece].reshape(rows, 2 * count)
        p[piece] = (dot(lhs[:, :count], both[0]) + dot(lhs[:, count:], both[1])).astype(BF16)

    with jax.named_scope("x_part1"):
        grad_b += x_part(0)
        grad_b += x_part(1)
        swap_grads(0, gx)
        grad_b += x_part(2)
        swap_grads(1, gz)
    with jax.named_scope("far_xz"):
        swaps[0].wait()
        partial(ring_x.src, t1, gx, (x + 2) % 4)
        ring_x.far()
        swaps[1].wait()
        partial(ring_z.src, t3, gz, (z + 4) % 8)
        ring_z.far()
    with jax.named_scope("x_part2"):
        grad_b += x_part(3)
        last = jnp.sum(dt * place_heads(p3), axis=0, keepdims=True) + jnp.exp(total) * place_heads(he)[0:1]
        p2 = place_heads(p2)
        dloga = dot(upper, p1 - dt * p2, lax.Precision.HIGHEST) + last
        draw = (p2 + decay_rate * dloga) * sig
        gy[0, :, 512:640] = grad_b.astype(BF16)
        gy[0, :, 640:768] = grad_c.astype(BF16)
        gy[0, :, 768:800] = draw[:, :32].astype(BF16)
        swap_grads(2, gy)
    with jax.named_scope("near"):
        for way in range(2):
            partial(ring_z.src, t3, gz, ring_z.piece(way, 3))
            ring_z.next_far(way)
        for step in (1, 3):
            partial(ring_x.src, t1, gx, (x + step) % 4)
            ring_x.near(step)
        swaps[2].wait()
        partial(ring_y.src, t2, gy, (y + 2) % 4)
        ring_y.far()
        for step in (1, 3):
            partial(ring_y.src, t2, gy, (y + step) % 4)
            ring_y.near(step)
        for s in (2, 1):
            for way in range(2):
                partial(ring_z.src, t3, gz, ring_z.piece(way, s))
    gt_v = r["gt_v"]

    def grad_tokens(k, carry):
        w = wbuf[k]
        cols = pl.ds(pl.multiple_of(k * 256, 256), 256)
        gt_v[:, cols] = (dot(gx[0], w[:WX]) + dot(gz[0], w[WX : WX + WZ]) + dot(gy[0], w[WX + WZ :])).astype(BF16)
        return carry

    with jax.named_scope("z3"):
        ring_z.long(3)
        partial(ring_x.src, t1, gx, x)
        partial(ring_z.src, t3, gz, z)
        partial(ring_y.src, t2, gy, y)
    with jax.named_scope("mid_x"):
        ring_x.middle()
        ring_z.short(2)
    with jax.named_scope("gt1"):
        lax.fori_loop(0, 2, grad_tokens, 0)
    with jax.named_scope("z2"):
        ring_z.long(2)
        ring_y.middle()
        ring_z.short(1)
    with jax.named_scope("gt2"):
        lax.fori_loop(2, 4, grad_tokens, 0)
    with jax.named_scope("z1"):
        ring_z.long(1)
    with jax.named_scope("gt3"):
        lax.fori_loop(4, 8, grad_tokens, 0)
        gt_copy = pltpu.make_async_copy(gt_v, r["gt_out"], r["in_sem"].at[1])
        gt_copy.start()

    ring_xy = Ring4(y, at.up, at.down, r["qx"], r["got_xy"], r["sxy"], r["rxy"])
    ring_yx = Ring4(x, at.right, at.left, r["qy"], r["got_yx"], r["syx"], r["ryx"])
    ring_zx = Ring4(x, at.right, at.left, r["qz"], r["got_zx"], r["szx"], r["rzx"])

    def onward(ring, nxt):
        q = nxt.src
        rows = q.shape[1]
        low, high = ring.end()
        for k in range(2):
            q[k] = low[k * rows : k * rows + rows].astype(BF16)
            q[k + 2] = high[k * rows : k * rows + rows].astype(BF16)
        nxt.far()
        nxt.near(1)
        nxt.near(3)

    with jax.named_scope("end_x"):
        onward(ring_x, ring_xy)
    with jax.named_scope("end_z"):
        onward(ring_z, ring_zx)
    with jax.named_scope("end_y"):
        onward(ring_y, ring_yx)
    with jax.named_scope("mids"):
        ring_xy.middle()
        ring_zx.middle()
        ring_yx.middle()
    along_z = [(d, (z + d) % 8, {"z": (z + d) % 8}) for d in range(1, 8)]
    along_y = [(d, (y + d) % 4, {"y": (y + d) % 4}) for d in range(1, 4)]
    lasts = []

    def scatter(ring, name, targets, lo):
        src, got, send, recv = (r[name + n] for n in ("_s", "_g", "_ss", "_rs"))
        low, high = ring.end()
        n = src.shape[0] // 2
        for k in range(n):
            src[k] = low[k * 8 : k * 8 + 8].astype(BF16)
            src[k + n] = high[k * 8 : k * 8 + 8].astype(BF16)
        for d, t, target in targets:
            copy = remote(src.at[t], got.at[d], send.at[d], recv.at[d], target)
            copy.start()
            copies.append(copy)
        lasts.append((src, got, send, recv, targets, lo))

    with jax.named_scope("scatter"):
        scatter(ring_xy, "fx", along_z, 0)
        scatter(ring_yx, "fy", along_z, WX + WZ)
        scatter(ring_zx, "fz", along_y, WX)
    gw = r["gw_out"]
    with jax.named_scope("finish"):
        for (src, got, send, recv, targets, lo), me in zip(lasts, (z, z, y)):
            out = src[me].astype(F32)
            for d, t, target in targets:
                remote(src.at[t], got.at[d], send.at[d], recv.at[d], target).wait_recv()
                out += got[d].astype(F32)
            gw[:, lo : lo + out.shape[1]] = out
        for ring in (ring_x, ring_y, ring_z, ring_xy, ring_yx, ring_zx):
            for copy in ring.copies:
                copy.wait_send()
        for copy in copies + gather.sends:
            copy.wait_send()
        y_copy.wait()
        gt_copy.wait()


def fused(tokens, w, a_log, dt_bias, d_skip, grad_y):
    count = tokens.shape[0]
    cols, depth = w.shape
    sd = jax.ShapeDtypeStruct
    dma = pltpu.SemaphoreType.DMA
    scratch = {
        "tok": ((count, 2048), BF16), "g": ((count, INNER), BF16), "wbuf": ((8, cols, depth), BF16), "acc": ((count, cols), F32),
        "tt": ((2, 4, 4, 64, count), F32), "tt3": ((2, 8, 128, count), F32),
        "tb": ((2, 4, 4, 64, count), BF16), "tb3": ((2, 8, 128, count), BF16),
        "tr": ((4, 4, 64, count), BF16), "tr3": ((8, 128, count), BF16),
        "t1": ((4, 4, 64, 2 * count), BF16), "t2": ((4, 4, 64, 2 * count), BF16), "t3": ((8, 128, 2 * count), BF16),
        "x": ((count, INNER), BF16), "y_v": ((count, INNER), BF16), "gt_v": ((count, 2048), BF16),
        "dte": ((count, INNER), F32), "ece": ((count, INNER), F32), "tle": ((count, INNER), F32),
        "cume": ((count, 2 * INNER), F32), "cumt": ((128, count), F32),
        "xdt": ((count, INNER), BF16), "xt": ((count, INNER), BF16), "gec": ((count, INNER), BF16),
        "yi": ((count, INNER), F32), "dxi": ((count, INNER), F32), "ds_acc": ((128, 128), F32),
        "stf": ((2, 2, 128, 1024), F32), "sst": ((2, 128, 1024), BF16), "pst": ((2, 128, 1024), BF16),
        "tot_s": ((8, 128), F32), "tot_r": ((8, 128), F32), "te": ((2, 2, 8, 1024), F32),
        "dmsg": ((8, 8, 128), F32), "dr": ((16, 8, 128), F32),
        "msg": ((2, 16, 64, 128), BF16), "rmsg": ((2, 16, 64, 128), BF16),
        "res": ((2, 16, 64, 128), BF16), "rres": ((2, 16, 64, 128), BF16),
        "se": ((2, 2, 128, 1024), BF16), "hs": ((2, 128, 1024), BF16), "ske": ((8, INNER), F32),
        "gx": ((2, count, WX), BF16), "gz": ((2, count, WZ), BF16), "gy": ((2, count, WY), BF16),
        "px": ((4, 256, WX), BF16), "py": ((4, 256, WY), BF16), "pz": ((8, 128, WZ), BF16),
        "got_x": ((6, 128, WX), BF16), "got_y": ((6, 128, WY), BF16), "got_z": ((16, 64, WZ), BF16),
        "qx": ((4, 64, WX), BF16), "qy": ((4, 64, WY), BF16), "qz": ((4, 32, WZ), BF16),
        "got_xy": ((6, 32, WX), BF16), "got_yx": ((6, 32, WY), BF16), "got_zx": ((6, 16, WZ), BF16),
        "fx_s": ((8, 8, WX), BF16), "fx_g": ((8, 8, WX), BF16), "fy_s": ((8, 8, WY), BF16), "fy_g": ((8, 8, WY), BF16),
        "fz_s": ((4, 8, WZ), BF16), "fz_g": ((4, 8, WZ), BF16),
    }
    sems = {
        "in_sem": (3,), "tok_sem": (4,), "g_send": (28,), "g_ici": (7, 4), "g_d2d_send": (7, 4), "g_d2d": (7, 4),
        "d_sem": (10,), "s0": (16,), "r0": (16,), "s1": (2, 16), "r1": (2, 16), "s2": (2, 16), "r2": (2, 16),
        "gs_sem": (3,), "gr_sem": (3,), "sx": (6,), "rx": (6,), "sy": (6,), "ry": (6,), "sz": (16,), "rz": (16,),
        "sxy": (6,), "rxy": (6,), "syx": (6,), "ryx": (6,), "szx": (6,), "rzx": (6,),
        "fx_ss": (8,), "fx_rs": (8,), "fy_ss": (8,), "fy_rs": (8,), "fz_ss": (4,), "fz_rs": (4,),
    }
    names = ["tokens", "w", "a_log", "dt_bias", "d_skip", "grad_y", "y_out", "gt_out", "gw_out", *scratch, *sems]

    def body(*refs):
        kernel(names, *refs)

    return pl.pallas_call(
        body,
        out_shape=(sd((count, INNER), BF16), sd((count, 2048), BF16), sd((8, cols), F32)),
        in_specs=[ANY, ANY, VM, VM, VM, ANY],
        out_specs=(ANY, ANY, VM),
        scratch_shapes=[pltpu.VMEM(*v) for v in scratch.values()] + [dma(v) for v in sems.values()],
        compiler_params=pltpu.CompilerParams(collective_id=0, has_side_effects=True, vmem_limit_bytes=LIMIT),
    )(tokens, w, a_log.reshape(1, -1), dt_bias.reshape(1, -1), d_skip.reshape(1, -1), grad_y)


def per_device(tokens, w_in, a_log, dt_bias, d_skip, grad_y):
    count, width = tokens.shape[1:]
    inner = grad_y.shape[2]
    y, gt, gw = fused(tokens.reshape(count, width), w_in.T, a_log, dt_bias, d_skip, grad_y.reshape(count, inner))
    return (y.reshape(1, count, inner), gt.reshape(1, count, width), gw)


def solution(mesh):
    torus = Mesh(mesh.devices.reshape(2, 8, 2, 2, 4), ("xh", "z", "c", "xl", "y"))
    placed = (P(ZERO, SEQ, None), P(ZERO, None), P(), P(), P(), P(ZERO, SEQ, None))
    return jax.shard_map(
        per_device,
        mesh=torus,
        in_specs=placed,
        out_specs=(P(ZERO, SEQ, None), P(ZERO, SEQ, None), P(SEQ + ZERO, None)),
        check_vma=False,
    )
```

time: 612 us -> 115 us (0.19)
  waiting for transfers between devices: 478 us -> 0 us
  Pallas kernels: 0 us -> 110 us
  blocking collectives: 39.3 us -> 0 us
  other arithmetic: 30.6 us -> 0 us
  matrix products: 28.6 us -> 0 us
  between operations: 14.7 us -> 0.66 us
  starting transfers between devices: 13.3 us -> 0 us
    all_gather x8 -> x0, waiting for transfers between devices: 428 us -> none  [the longest x6 266 us: prefix_by_axis(): pieces = jax.tree.map(lambda part: lax.all_gather(part, axis), so_far)]
    pallas_call x0 -> x1, Pallas kernels: none -> 110 us  [fused(): pl.pallas_call(body, out_shape=(sd((count, INNER), BF16), sd((count, 2048...]
    all_to_all x1 -> x0, waiting for transfers between devices: 48.9 us -> none  [summed_on_arrival(): blocks = lax.all_to_all(cut_along(array, dim, size), axis, 0, 0, tiled=True)]
    dot_general x16 -> x0, matrix products: 28.6 us -> none  [the longest x1 6.12 us: per_device(): lax.dot_general(gproj, full_w, (((1,), (1,)), ((), ())), preferred_elemen...]
    all_gather x4 -> x0, blocking collectives: 27 us -> none  [prefix_by_axis(): pieces = jax.tree.map(lambda part: lax.all_gather(part, axis), so_far)]
    add x4 -> x0, other arithmetic: 14.8 us -> none  [the longest x2 7.47 us: carry_backward(): later[1] + jnp.exp(later[0])[:, None, None] * earlier[1]]
    all_to_all x1 -> x0, starting transfers between devices: 13 us -> none  [summed_on_arrival(): blocks = lax.all_to_all(cut_along(array, dim, size), axis, 0, 0, tiled=True)]
    reduce_sum x4 -> x0, other arithmetic: 12.5 us -> none  [the longest x1 10.4 us: block_ssd(): jnp.exp(cum[-1])[:, None, None] * start]
  transfers between devices with their start and end apart: 9 -> 0, of which waited for: 9 -> 0; matrix products, arithmetic and copies ran while one was open for 5% -> 0% of each run, Pallas kernels for 0% -> 0%
where the time goes in v2:
time: 115 us; the launch traced here: 114 us
  Pallas kernels  110 us (96%)
  local copies, waits for them, and re-layouts  3.38 us (3%)
    pallas_call x1, Pallas kernels, fused(): pl.pallas_call(body, out_shape=(sd((count, INNER), BF16), sd((count, 2048...  110 us
    unnamed x7, local copies, waits for them, and re-layouts  3.38 us

profile of v2, /device:TPU:1, one launch (start us, length us, event | category | flops | bytes accessed | tf_op | source)
XLA Modules:
  0.0 114.4 jit_solution(718596854519730046)
XLA Ops:
  0.6 110.4 %shard_map.85 = (bf16[128,2048]{1,0:T(8,128)(2,1)}, bf16[128,2048]{1,0:T(8,128)(2,1)}, f32[8,2336]{1,0:T(8,128)}) custom-call(bf16[128,2048]{1,0:T(8,128)(2,1)} %bitcast.9, bf16[2336,256]{1,0:T(8,128)(2,1)} %bitcast.8, f32[1,32]{1,0:T(1,128)} %bitcast.13, f32[1,32]{1,0:T(1,128)} %bitcast.14, f32[1,32]{1,0:T(1,128)} %bitcast.15, bf16[128,2048]{1,0:T(8,128)(2,1)} %bitcast.10), custom_call_target="tpu_custom_call" | custom-call | tf_op jit(solution)/shard_map/pallas_call | solution.py:775
  111.0 0.0 copy-start
  111.0 0.0 copy-start.1
  111.0 1.9 %copy.12 = bf16[1,128,2048]{2,1,0:T(8,128)(2,1)} copy(bf16[1,128,2048]{2,1,0:T(8,128)(2,1)} %bitcast.12) | data formatting | bytes 1048576
  113.0 0.0 copy-done
  113.0 0.8 copy.13
  113.8 0.0 copy-done.1
  113.8 0.6 copy.14
Async XLA Ops:
  111.0 2.0 %copy-start = (bf16[128,2048]{1,0:T(8,128)(2,1)S(1)}, bf16[128,2048]{1,0:T(8,128)(2,1)}, u32[]{:S(2)}) copy-start(bf16[128,2048]{1,0:T(8,128)(2,1)} %get-tuple-element.7) | copy-start | bytes 1572868
  111.0 2.8 %copy-start.1 = (f32[8,2336]{1,0:T(8,128)S(1)}, f32[8,2336]{1,0:T(8,128)}, u32[]{:S(2)}) copy-start(f32[8,2336]{1,0:T(8,128)} %get-tuple-element.14) | copy-start | bytes 224260

commit v3 on v2

v3 whole, which is shorter than its diff:
```python
from types import SimpleNamespace

import jax
import jax.numpy as jnp
from jax import lax
from jax.experimental import pallas as pl
from jax.experimental.pallas import tpu as pltpu
from jax.sharding import Mesh
from jax.sharding import PartitionSpec as P

SEQ = ("xh", "z", "c")
ZERO = ("xl", "y")
MESH = pl.DeviceIdType.MESH
F32 = jnp.float32
BF16 = jnp.bfloat16
LIMIT = 62 * 1024 * 1024
VM = pl.BlockSpec(memory_space=pltpu.VMEM)
ANY = pl.BlockSpec(memory_space=pl.ANY)
INNER = 2048
EDGE_SMALL, EDGE_LARGE = 384, 400
WA, WZ, WB, WV = 1024, 384, 768, 160


def remote(src, dst, send, recv, target):
    return pltpu.make_async_remote_copy(
        src_ref=src, dst_ref=dst, send_sem=send, recv_sem=recv, device_id=target, device_id_type=MESH
    )


def sent(block, sem, target):
    remote(block, block, sem, sem, target).wait_send()


def received(block, sem, target):
    remote(block, block, sem, sem, target).wait_recv()


def along_x(x):
    return {"xh": x // 2, "xl": x % 2}


def dot(a, b, precision=None):
    return jnp.dot(a, b, preferred_element_type=F32, precision=precision)


def dot_nt(a, b):
    return lax.dot_general(a, b, (((1,), (1,)), ((), ())), preferred_element_type=F32)


class Place:
    def __init__(self):
        self.xh, self.z, self.c, self.xl, self.y = (lax.axis_index(a) for a in ("xh", "z", "c", "xl", "y"))
        self.x = self.xh * 2 + self.xl
        self.chip = self.xh * 8 + self.z
        self.right, self.left = along_x((self.x + 1) % 4), along_x((self.x + 3) % 4)
        self.up, self.down = {"y": (self.y + 1) % 4}, {"y": (self.y + 3) % 4}
        self.fore, self.aft = {"z": (self.z + 1) % 8}, {"z": (self.z + 7) % 8}
        self.mate = {"c": 1 - self.c}
        self.others = []
        for d in (4, 12, 3, 5, 11, 13, 2, 6, 10, 14, 8, 1, 7, 9, 15):
            t = (self.chip + d) % 16
            self.others.append((d, t, (self.chip + 16 - d) % 16, {"xh": t // 8, "z": t % 8}))

    def greet(self):
        barrier = pltpu.get_barrier_semaphore()
        targets = [self.mate, self.right, self.left, self.up, self.down, {"y": (self.y + 2) % 4}] + [o[3] for o in self.others]
        for target in targets:
            pl.semaphore_signal(barrier, inc=1, device_id=target, device_id_type=MESH)
        pl.semaphore_wait(barrier, len(targets))


class Gather:
    def __init__(self, at, w, wbuf, s):
        self.at, self.w, self.wbuf, self.s = at, w, wbuf, s
        self.rel = [self.shard(0, 3), self.shard(0, 1), self.shard(0, 2)] + [self.shard(1, d) for d in (0, 3, 1, 2)]
        self.mine = self.shard(0, 0)

    def shard(self, flip, dy):
        return (self.at.xl + flip) % 2 * 4 + (self.at.y + dy) % 4

    def rows(self, part, core=None):
        core = self.at.c if core is None else core
        odd = self.at.z % 2
        base = core * (2 * EDGE_SMALL + EDGE_LARGE)
        far = EDGE_SMALL + EDGE_LARGE
        if part == "a":
            start, size = base + odd * far, EDGE_SMALL
        elif part == "b":
            start, size = base + EDGE_SMALL, EDGE_LARGE
        elif part in ("a0", "a1"):
            start, size = base + odd * far + (part == "a1") * (EDGE_SMALL // 2), EDGE_SMALL // 2
        else:
            start, size = base + (1 - odd) * far, EDGE_SMALL
        return pl.ds(pl.multiple_of(start, 16), size)

    def block(self, k, part, core=None):
        return self.wbuf.at[k, self.rows(part, core)]

    def send(self, k, part, to, slot, lane):
        block = self.block(k, part)
        remote(block, block, self.s.g_send.at[0], self.s.g_ici.at[slot, lane], to).start()

    def depth_send(self, k, slot):
        self.send(k, "a0", self.at.fore, slot, 2)
        self.send(k, "a1", self.at.aft, slot, 2)

    def begin(self):
        at = self.at
        self.send(self.mine, "a", at.up, 0, 0)
        self.send(self.mine, "b", at.down, 1, 1)
        self.send(self.mine, "a", at.left, 3, 0)
        self.send(self.mine, "b", at.right, 3, 1)
        self.send(self.mine, "b", at.up, 0, 1)
        self.send(self.mine, "a", at.down, 1, 0)

    def arrive(self, slot, lane):
        block = self.block(self.rel[slot], ("a", "b", "m")[lane])
        received(block, self.s.g_ici.at[slot, lane], self.at.mate)
        remote(block, block, self.s.g_send.at[0], self.s.g_d2d.at[slot], self.at.mate).start()

    def a(self, slot, *onward):
        self.arrive(slot, 0)
        for to, there in onward:
            self.send(self.rel[slot], "a", to, there, 0)
        self.depth_send(self.rel[slot], slot)

    def b(self, slot, *onward):
        self.arrive(slot, 1)
        for to, there in onward:
            self.send(self.rel[slot], "b", to, there, 1)

    def m(self, slot):
        self.arrive(slot, 2)

    def whole(self, slot):
        half = self.wbuf.shape[1] // 2
        rows = pl.ds(pl.multiple_of((1 - self.at.c) * half, 16), half)
        received(self.wbuf.at[self.rel[slot], rows], self.s.g_d2d.at[slot], self.at.mate)

    def end(self):
        sent(self.wbuf.at[pl.ds(0, 7)], self.s.g_send.at[0], self.at.mate)


def spread(row):
    lane = lax.broadcasted_iota(jnp.int32, (row.shape[0], 128), 1)
    out = []
    for j in range(16):
        out.append(jnp.where(lane < 64, row[:, 2 * j : 2 * j + 1], row[:, 2 * j + 1 : 2 * j + 2]))
    return out


def heads(values, part):
    high = values.astype(BF16)
    low = (values - high.astype(F32)).astype(BF16)
    return dot(high, part) + dot(low, part)


class Share:
    def __init__(self, plus, minus, mate, g, lhs, acc, send, ici, d2d):
        self.plus, self.minus, self.mate, self.g, self.lhs, self.acc = plus, minus, mate, g, lhs, acc
        self.sem, self.ici, self.d2d = send, ici, d2d
        self.h = g.shape[1] // 2

    def half(self, n, part):
        return self.g.at[n, pl.ds(part * self.h, self.h)]

    def go(self, src, slot, part, to):
        remote(self.half(src, part), self.half(2 * slot, part), self.sem, self.ici.at[slot, part], to).start()

    def begin(self):
        remote(self.g.at[0], self.g.at[1], self.sem, self.d2d.at[0], self.mate).start()
        self.go(0, 3, 0, self.plus)
        self.go(0, 1, 1, self.minus)
        self.go(0, 3, 1, self.plus)
        self.go(0, 1, 0, self.minus)

    def arrive(self, slot, part):
        received(self.half(2 * slot, part), self.ici.at[slot, part], self.plus)
        block = self.half(2 * slot, part)
        remote(block, self.half(2 * slot + 1, part), self.sem, self.d2d.at[slot], self.mate).start()

    def early(self):
        self.arrive(3, 0)
        self.go(6, 2, 0, self.plus)
        self.arrive(1, 1)
        self.go(2, 2, 1, self.minus)

    def near(self):
        self.arrive(3, 1)
        self.arrive(1, 0)

    def far(self):
        self.arrive(2, 0)
        self.arrive(2, 1)

    def product(self, slot):
        received(self.g.at[2 * slot + 1], self.d2d.at[slot], self.mate)
        rhs = self.g[2 * slot : 2 * slot + 2].reshape(4 * self.h, self.g.shape[2])
        value = dot(self.lhs[slot], rhs)
        self.acc[...] = value if slot == 0 else self.acc[...] + value

    def end(self):
        h = self.acc.shape[0] // 2
        return self.acc[:h], self.acc[h:]

    def drain(self):
        sent(self.g.at[pl.ds(0, 7)], self.sem, self.mate)


class Scatter:
    def __init__(self, me, targets, src, got, send, recv):
        self.me, self.targets, self.src, self.got, self.sem, self.recv = me, targets, src, got, send, recv

    def begin(self, low, high):
        n, rows = self.src.shape[0] // 2, self.src.shape[1]
        for k in range(n):
            self.src[k] = low[k * rows : k * rows + rows].astype(BF16)
            self.src[k + n] = high[k * rows : k * rows + rows].astype(BF16)
        for d, t, target in self.targets:
            remote(self.src.at[t], self.got.at[d], self.sem, self.recv, target).start()

    def all(self):
        return self.got.at[pl.ds(1, len(self.targets))]

    def end(self):
        received(self.all(), self.recv, self.targets[0][2])
        out = self.src[self.me].astype(F32)
        for d in range(1, len(self.targets) + 1):
            out += self.got[d].astype(F32)
        return out

    def halves(self):
        out = self.end()
        h = out.shape[0] // 2
        return out[:h], out[h:]

    def drain(self):
        sent(self.all(), self.sem, self.targets[0][2])


class Ring8:
    def __init__(self, me, plus, minus, src, got, send, recv):
        self.me, self.src, self.got, self.sem, self.recv = me, src, got, send, recv
        self.to = (plus, minus)
        self.h = src.shape[1] // 2

    def piece(self, way, s):
        return (self.me + (s if way == 0 else 8 - s)) % 8

    def slot(self, way, half, s):
        return (way * 2 + half) * 4 + s

    def go(self, way, half, s):
        block = self.src.at[self.piece(way, s), pl.ds(half * self.h, self.h)]
        n = self.slot(way, half, s - 1)
        remote(block, self.got.at[n], self.sem, self.recv.at[n], self.to[way]).start()

    def landed(self, way, half, s):
        n = self.slot(way, half, s)
        received(self.got.at[n], self.recv.at[n], self.to[way])
        return self.got[n].astype(F32)

    def on(self, way, half, s):
        at = self.piece(way, s)
        rows = slice(half * self.h, half * self.h + self.h)
        self.src[at, rows] = (self.src[at, rows].astype(F32) + self.landed(way, half, s)).astype(BF16)
        self.go(way, half, s)

    def far(self):
        self.go(0, 0, 4)
        self.go(1, 1, 4)

    def next_far(self, way):
        self.go(way, 1 - way, 3)

    def long(self, s):
        self.on(0, 0, s)
        self.on(1, 1, s)

    def short(self, s):
        self.on(0, 1, s)
        self.on(1, 0, s)

    def end(self):
        low = self.src[self.me, : self.h].astype(F32) + self.landed(1, 0, 0)
        high = self.src[self.me, self.h :].astype(F32) + self.landed(0, 1, 0)
        return low + self.landed(0, 0, 0), high + self.landed(1, 1, 0)

    def drain(self):
        sent(self.got.at[pl.ds(0, 14)], self.sem, self.to[0])


def kernel(r):
    at = Place()
    c, x, y, z, chip, mate = at.c, at.x, at.y, at.z, at.chip, at.mate
    first = c == 0
    own = pl.ds(c, 1)

    tok, acc, wbuf = r.tok, r.acc, r.wbuf
    count = tok.shape[0]
    depth = wbuf.shape[2]
    gather = Gather(at, r.w, wbuf, r)
    w_copy = pltpu.make_async_copy(r.w, wbuf.at[gather.mine], r.in_sem.at[0])
    tok_copy = pltpu.make_async_copy(r.tokens, tok, r.in_sem.at[1])
    g_copy = pltpu.make_async_copy(r.grad_y, r.g, r.in_sem.at[2])
    w_copy.start()
    tok_copy.start()
    g_copy.start()
    with jax.named_scope("greet"):
        at.greet()
    w_copy.wait()
    gather.begin()
    tok_copy.wait()
    scope_tok = jax.named_scope("tok")
    scope_tok.__enter__()
    tt, tt3 = r.tt, r.tt3
    for i in range(16):
        block = tok[:, i * 128 : (i + 1) * 128].astype(F32).T
        for n in range(16):
            core, xlow, yy = n // 8, n // 4 % 2, n % 4
            rows = block[n * 8 : n * 8 + 8, :]
            xx, zz = i // 8 * 2 + xlow, i % 8
            tt[core, xx, yy, zz * 8 : zz * 8 + 8, :] = rows
            tt3[core, zz, xx * 32 + yy * 8 : xx * 32 + yy * 8 + 8, :] = rows
    tb, tb3, tr, tr3 = r.tb, r.tb3, r.tr, r.tr3
    tb[...] = tt[...].astype(BF16)
    tb3[...] = tt3[...].astype(BF16)
    swap = remote(tb.at[1 - c], tr, r.tok_sem.at[0], r.tok_sem.at[1], mate)
    swap3 = remote(tb3.at[1 - c], tr3, r.tok_sem.at[2], r.tok_sem.at[3], mate)
    swap.start()
    swap3.start()
    t1, t2, t3 = r.t1, r.t2, r.t3

    def place_rows(lo, one, three):
        t3[:, :, lo : lo + 128] = three
        for i in range(4):
            for j in range(4):
                t1[i, j * 64 : j * 64 + 64, lo : lo + 128] = one[i, j]
                t2[j, i * 64 : i * 64 + 64, lo : lo + 128] = one[i, j]

    place_rows(0, tb[own][0], tb3[own][0])
    acc[...] = jnp.zeros_like(acc)

    def multiply(*ks):
        def body(i, carry):
            k = ks[0]
            for n in range(1, len(ks)):
                k = jnp.where(i == n, ks[n], k)
            acc[...] += dot_nt(tok[:, pl.ds(pl.multiple_of(k * depth, depth), depth)], wbuf[k])
            return carry

        lax.fori_loop(0, len(ks), body, 0)

    scope_tok.__exit__(None, None, None)
    ga, gb, gm, rel = gather.a, gather.b, gather.m, gather.rel
    with jax.named_scope("g1"):
        ga(0, (at.up, 2), (at.left, 4))
        gb(1, (at.down, 2), (at.right, 5))
        ga(3)
        gb(3)
    with jax.named_scope("g2"):
        gb(0, (at.right, 4))
        ga(1, (at.left, 5))
        ga(4)
        gb(5)
        gm(0)
        gm(3)
    with jax.named_scope("g3"):
        ga(2, (at.left, 6))
        gb(2, (at.right, 6))
        gb(4)
        ga(5)
        gather.whole(0)
        gather.whole(3)
        multiply(gather.mine, rel[0], rel[3])
    with jax.named_scope("g4"):
        gm(1)
        gm(4)
        ga(6)
        gb(6)
        gm(2)
        gm(5)
        gather.whole(1)
        gather.whole(4)
        multiply(rel[1], rel[4])
    with jax.named_scope("g5"):
        gm(6)
        gather.whole(2)
        gather.whole(5)
        multiply(rel[2], rel[5])
    with jax.named_scope("g6"):
        swap.wait()
        swap3.wait()
        gather.whole(6)
    with jax.named_scope("g7"):
        multiply(rel[6])

    x_r, g_r = r.x, r.g
    dte, ece, tle, cume, cumt = r.dte, r.ece, r.tle, r.cume, r.cumt
    xdt, xt, gec, yi, dxi, ds_acc = r.xdt, r.xt, r.gec, r.yi, r.dxi, r.ds_acc
    stf, sst, pst, te, ske = r.stf, r.sst, r.pst, r.te, r.ske
    tot_s, tot_r, dmsg, dr = r.tot_s, r.tot_r, r.dmsg, r.dr
    msg, rmsg, res, rres, se, hs = r.msg, r.rmsg, r.res, r.rres, r.se, r.hs
    d_sem = r.d_sem
    copies = []
    with jax.named_scope("prep"):
        bm = acc[:, INNER : INNER + 128].astype(BF16)
        cm = acc[:, INNER + 128 : INNER + 256].astype(BF16)
        rowz = jnp.zeros((1, 96), F32)
        decay_rate = jnp.concatenate([-jnp.exp(r.a_log[...]), rowz], axis=1)
        bias = jnp.concatenate([r.dt_bias[...], rowz], axis=1)
        u = jnp.concatenate([acc[:, INNER + 256 :], jnp.zeros((count, 96), F32)], axis=1) + bias
        small = jnp.exp(-jnp.abs(u))
        dt = jnp.maximum(u, 0.0) + jnp.log1p(small)
        sig = jnp.where(u >= 0, 1.0, small) / (1.0 + small)
        ti = lax.broadcasted_iota(jnp.int32, (128, 128), 0)
        si = lax.broadcasted_iota(jnp.int32, (128, 128), 1)
        keep, keep_t = ti >= si, ti <= si
        lower = jnp.where(keep, 1.0, 0.0).astype(F32)
        upper = jnp.where(keep_t, 1.0, 0.0).astype(F32)
        cum = dot(lower, decay_rate * dt, lax.Precision.HIGHEST)
        total = cum[127:128, :]
        tot_s[...] = jnp.broadcast_to(total, (8, 128))
        tot_copy = remote(tot_s, tot_r, d_sem.at[0], d_sem.at[1], mate)
        tot_copy.start()
        lane = lax.broadcasted_iota(jnp.int32, (count, 128), 1)

        def widen(arr, dst):
            for j, e in enumerate(spread(arr)):
                dst[:, j * 128 : (j + 1) * 128] = e

        widen(jnp.exp(cum), ece)
        g_copy.wait()
        gec[...] = (g_r[...].astype(F32) * ece[...]).astype(BF16)
        ct = cm.astype(F32).T.astype(BF16)

    def local_states(kind, lhs, rhs):
        for half in range(2):
            stf[kind, half] = dot(lhs, rhs[:, half * 1024 : half * 1024 + 1024])
        sst[kind] = stf[kind, pl.ds(1 - c, 1)][0].astype(BF16)
        copy = remote(sst.at[kind], pst.at[kind], d_sem.at[2 + 2 * kind], d_sem.at[3 + 2 * kind], mate)
        copy.start()
        return copy

    with jax.named_scope("states"):
        st_b = local_states(1, ct, gec)
        widen(dt, dte)
        widen(jnp.exp(total - cum), tle)
        xs = acc[:, :INNER].astype(BF16)
        x_r[...] = xs
        xd = xs.astype(F32) * dte[...]
        xdt[...] = xd.astype(BF16)
        xt[...] = (xd * tle[...]).astype(BF16)
        bt = bm.astype(F32).T.astype(BF16)
        st_copies = [local_states(0, bt, xt), st_b]
        tot_copy.wait()
        for n, arr in enumerate((tot_s, tot_r)):
            for j, e in enumerate(spread(arr[...])):
                te[n, j // 8, :, j % 8 * 128 : j % 8 * 128 + 128] = e
        for j in range(8):
            l = slice(j * 128, j * 128 + 128)
            dmsg[j] = te[0, own, :, l][0] + te[1, own, :, l][0]
        dr[pl.ds(chip, 1)] = dmsg[pl.ds(chip // 2, 1)]
        for d, t, source, target in at.others:
            remote(dmsg.at[t // 2], dr.at[chip], r.s_scan.at[0], r.r_scan.at[0], target).start()
        e_own, e_mate = jnp.exp(te[0, own][0][0:1]), jnp.exp(te[1, own][0][0:1])
        e0 = jnp.where(first, e_own, e_mate)
        e1 = jnp.where(first, e_mate, e_own)

    def send_states(kind):
        st_copies[kind].wait()
        mine, theirs = stf[kind, own][0], pst[kind].astype(F32)
        early = jnp.where(first, mine, theirs)
        late = jnp.where(first, theirs, mine)
        whole = (e1 * early + late if kind == 0 else early + e0 * late).astype(BF16)
        for i in range(16):
            msg[kind, i] = whole[i % 2 * 64 : i % 2 * 64 + 64, i // 2 * 128 : i // 2 * 128 + 128]
        for d, t, source, target in at.others:
            remote(msg.at[kind, t], rmsg.at[kind, chip], r.s_scan.at[1 + kind], r.r_scan.at[1 + kind], target).start()
        rmsg[kind, pl.ds(chip, 1)] = msg[kind, pl.ds(chip, 1)]

    def scan_states(kind):
        if kind == 1:
            received(dr.at[pl.ds(0, 15)], r.r_scan.at[0], mate)
        received(rmsg.at[kind, pl.ds(0, 15)], r.r_scan.at[1 + kind], mate)
        state = jnp.zeros((64, 128), F32)
        for i in range(16) if kind == 0 else reversed(range(16)):
            res[kind, i] = state.astype(BF16)
            state = jnp.exp(dr[i][0:1]) * state + rmsg[kind, i].astype(F32)
        for d, t, source, target in at.others:
            remote(res.at[kind, t], rres.at[kind, chip], r.s_scan.at[3 + kind], r.r_scan.at[3 + kind], target).start()
        rres[kind, pl.ds(chip, 1)] = res[kind, pl.ds(chip, 1)]

    def take_states(kind):
        received(rres.at[kind, pl.ds(0, 15)], r.r_scan.at[3 + kind], mate)
        for j in range(8):
            l = slice(j * 128, j * 128 + 128)
            got = jnp.concatenate([rres[kind, 2 * j], rres[kind, 2 * j + 1]], axis=0).astype(F32)
            mine, theirs = stf[kind, own, :, l][0], pst[kind, :, l].astype(F32)
            if kind == 0:
                edge, inside = got, e0[:, l] * got + jnp.where(first, mine, theirs)
                low, high = edge, inside
            else:
                edge, inside = got, jnp.where(first, theirs, mine) + e1[:, l] * got
                low, high = inside, edge
            se[kind, own, :, l] = jnp.where(first, low, high).astype(BF16)[None]
            hs[kind, :, l] = jnp.where(first, high, low).astype(BF16)
        copy = remote(hs.at[kind], se.at[kind, c], d_sem.at[6 + 2 * kind], d_sem.at[7 + 2 * kind], mate)
        copy.start()
        copies.append(copy)

    def mate_states(kind):
        remote(hs.at[kind], se.at[kind, 1 - c], d_sem.at[6 + 2 * kind], d_sem.at[7 + 2 * kind], mate).wait_recv()

    with jax.named_scope("send_b"):
        send_states(1)
    with jax.named_scope("send_f"):
        send_states(0)

    with jax.named_scope("pairs_prep"):
        cumt[...] = cum.T
        scores = dot_nt(cm, bm)
        scores_t = dot_nt(bm, cm)
        ds_acc[...] = jnp.zeros_like(ds_acc)
        for j, e in enumerate(spread(jnp.broadcast_to(jnp.concatenate([r.d_skip[...], rowz], axis=1), (8, 128)))):
            ske[:, j * 128 : (j + 1) * 128] = e
        for h in range(32):
            cume[:, h * 128 : h * 128 + 128] = jnp.broadcast_to(cum[:, h : h + 1], (count, 128))

    def pair(j, carry):
        cols = pl.ds(pl.multiple_of(j * 128, 128), 128)
        xj = xdt[:, cols]
        gj = g_r[:, cols]
        none = jnp.zeros_like(xj)
        xx = jnp.concatenate([jnp.where(lane < 64, xj, none), jnp.where(lane < 64, none, xj)], axis=0)
        gg = jnp.concatenate([jnp.where(lane < 64, gj, none), jnp.where(lane < 64, none, gj)], axis=0)
        ww = dot_nt(gg, xj)
        mix, mix_t = [], []
        total_ds = ds_acc[...]
        for n in range(2):
            span = cume[:, pl.ds(pl.multiple_of(j * 256 + n * 128, 128), 128)] - cumt[pl.ds(2 * j + n, 1), :]
            decay = jnp.exp(jnp.where(keep, span, -1e30))
            decay_t = jnp.exp(jnp.where(keep_t, -span, -1e30))
            mix.append((scores * decay).astype(BF16))
            mix_t.append((scores_t * decay_t).astype(BF16))
            total_ds += ww[n * 128 : n * 128 + 128] * decay
        ds_acc[...] = total_ds
        yi[:, cols] = dot(jnp.concatenate(mix, axis=1), xx)
        dxi[:, cols] = dot(jnp.concatenate(mix_t, axis=1), gg)
        return carry

    by_y = [(d, (y + d) % 4, {"y": (y + d) % 4}) for d in (2, 1, 3)]
    by_x = [(d, (x + d) % 4, along_x((x + d) % 4)) for d in (2, 1, 3)]
    with jax.named_scope("pairs1"):
        place_rows(128, tr[...], tr3[...])
        for n, (t, l, me, targets) in enumerate(((t2, r.ly, y, by_y), (t1, r.lx, x, by_x))):
            for d, to, target in targets:
                remote(t.at[to], l.at[4 - d], r.t_sem.at[n], r.t_sem.at[2 + n], target).start()
            l[0] = t[me]
        lax.fori_loop(0, 6, pair, 0)
    with jax.named_scope("scan_b"):
        scan_states(1)
    with jax.named_scope("pairs2"):
        lax.fori_loop(6, 11, pair, 0)
    with jax.named_scope("scan_f"):
        scan_states(0)
    with jax.named_scope("pairs3"):
        lax.fori_loop(11, 16, pair, 0)
        ds = ds_acc[...]
        ds_t = ds.T.astype(BF16)
        ds = ds.astype(BF16)
        grad_c = dot(ds, bm)
        grad_b = dot(ds_t, cm)
    segment = jnp.where(
        lax.broadcasted_iota(jnp.int32, (512, 128), 0) // 64 == lax.broadcasted_iota(jnp.int32, (512, 128), 1), 1.0, 0.0
    ).astype(BF16)
    y_v = r.y_out

    def place_heads(arrs):
        lane8 = lax.broadcasted_iota(jnp.int32, arrs[0].shape, 1)
        out = arrs[0]
        for q in range(1, 4):
            out = jnp.where(lane8 < 8 * q, out, pltpu.roll(arrs[q], 8 * q, 1))
        return out

    with jax.named_scope("take_b"):
        take_states(1)
        mate_states(1)

    ga, gz, gb, gv = r.ga, r.gz, r.gb, r.gv
    p2, p3 = [], []

    def x_part(q):
        half, l = q // 2, slice(q % 2 * 512, q % 2 * 512 + 512)
        cols = slice(q * 512, q * 512 + 512)
        en = se[1, half, :, l]
        xs = x_r[:, cols].astype(F32)
        dxs = tle[:, cols] * dot(bm, en)
        dxn = dxi[:, cols] + dxs
        dx = (dte[:, cols] * dxn + ske[0:1, cols] * g_r[:, cols].astype(F32)).astype(BF16)
        if q < 2:
            ga[0, :, q * 512 : q * 512 + 512] = dx
        elif q == 2:
            gz[0, :, :] = dx[:, :WZ]
            gb[0, :, :128] = dx[:, WZ:]
        else:
            gb[0, :, 128:640] = dx
        p2.append(heads(xs * dxn, segment))
        p3.append(heads(xs * dxs, segment))
        return dot_nt(xt[:, cols], en)

    share_a = Share(at.up, at.down, mate, ga, r.ly, r.acc_a, r.s_share.at[0], r.r_share.at[0], r.d_share.at[0])
    share_b = Share(at.right, at.left, mate, gb, r.lx, r.acc_b, r.s_share.at[1], r.r_share.at[1], r.d_share.at[1])
    share_v = Share(at.up, at.down, mate, gv, r.ly, r.acc_v, r.s_share.at[2], r.r_share.at[2], r.d_share.at[2])
    ring_z = Ring8(z, at.fore, at.aft, r.pz, r.got_z, r.s_share.at[3], r.rz)

    def partial(p, lhs, both, piece):
        rows = p.shape[1]
        lhs = lhs[piece].reshape(rows, 2 * count)
        p[piece] = dot(lhs, both[...].reshape(2 * count, p.shape[2])).astype(BF16)

    with jax.named_scope("x_part"):
        grad_b += x_part(0)
        grad_b += x_part(1)
        share_a.begin()
        grad_b += x_part(2)
        swap_z = remote(gz.at[0], gz.at[1], d_sem.at[10], d_sem.at[11], mate)
        swap_z.start()
        grad_b += x_part(3)
        gb[0, :, 640:] = grad_b.astype(BF16)
        share_b.begin()
    with jax.named_scope("far_z"):
        swap_z.wait()
        partial(ring_z.src, t3, gz, (z + 4) % 8)
        ring_z.far()
        for way in range(2):
            partial(ring_z.src, t3, gz, ring_z.piece(way, 3))
            ring_z.next_far(way)
        for s in (2, 1):
            for way in range(2):
                partial(ring_z.src, t3, gz, ring_z.piece(way, s))
        partial(ring_z.src, t3, gz, z)
    with jax.named_scope("take_f"):
        take_states(0)
    with jax.named_scope("early"):
        share_a.early()
        share_b.early()
    with jax.named_scope("z3"):
        ring_z.long(3)
    with jax.named_scope("mate_f"):
        mate_states(0)
    with jax.named_scope("y_part"):
        p1, he = [], []
        for q in range(4):
            half, l = q // 2, slice(q % 2 * 512, q % 2 * 512 + 512)
            cols = slice(q * 512, q * 512 + 512)
            st = se[0, half, :, l]
            xs = x_r[:, cols].astype(F32)
            yo = yi[:, cols] + ece[:, cols] * dot(cm, st)
            y_v[:, cols] = (yo + ske[0:1, cols] * xs).astype(BF16)
            p1.append(heads(g_r[:, cols].astype(F32) * yo, segment))
            both = jnp.sum(se[1, half, :, l].astype(F32) * st.astype(F32), axis=0, keepdims=True)
            he.append(heads(jnp.broadcast_to(both, (8, 512)), segment))
            grad_c += dot_nt(gec[:, cols], st)
        p1, p2 = place_heads(p1), place_heads(p2)
        last = jnp.sum(dt * place_heads(p3), axis=0, keepdims=True) + jnp.exp(total) * place_heads(he)[0:1]
        dloga = dot(upper, p1 - dt * p2, lax.Precision.HIGHEST) + last
        draw = (p2 + decay_rate * dloga) * sig
        gv[0, :, :128] = grad_c.astype(BF16)
        gv[0, :, 128:] = draw[:, :32].astype(BF16)
        share_v.begin()
    gt_v = r.gt_out

    def grad_tokens(k, carry):
        w = wbuf[k]
        cols = pl.ds(pl.multiple_of(k * 256, 256), 256)
        out = dot(ga[0], w[:WA]) + dot(gz[0], w[WA : WA + WZ])
        out += dot(gb[0], w[WA + WZ : WA + WZ + WB]) + dot(gv[0], w[WA + WZ + WB :])
        gt_v[:, cols] = out.astype(BF16)
        return carry

    with jax.named_scope("near"):
        share_a.near()
        share_b.near()
        ring_z.short(2)
        ring_z.long(2)
    with jax.named_scope("prod"):
        for n, l in ((0, r.ly), (1, r.lx)):
            received(l.at[pl.ds(1, 3)], r.t_sem.at[2 + n], mate)
        for slot in (0, 3, 1):
            share_a.product(slot)
            share_b.product(slot)
    with jax.named_scope("far"):
        share_v.early()
        share_a.far()
        share_b.far()
        ring_z.short(1)
        share_v.near()
        ring_z.long(1)

    by_z = [(d, (z + d) % 8, {"z": (z + d) % 8}) for d in (4, 3, 5, 2, 6, 1, 7)]
    def scatter(n, me, targets, src, got):
        return Scatter(me, targets, src, got, r.s_last.at[n], r.r_last.at[n])

    mid_a = scatter(0, x, by_x, r.qa, r.got_a)
    mid_b = scatter(1, y, by_y, r.qb, r.got_b)
    mid_v = scatter(2, x, by_x, r.qv, r.got_v)
    mid_z = scatter(3, x, by_x, r.qz, r.got_zx)
    end_a = scatter(4, z, by_z, r.fa_s, r.fa_g)
    end_b = scatter(5, z, by_z, r.fb_s, r.fb_g)
    end_v = scatter(6, z, by_z, r.fv_s, r.fv_g)
    end_z = scatter(7, y, by_y, r.fz_s, r.fz_g)
    with jax.named_scope("end_a"):
        share_a.product(2)
        mid_a.begin(*share_a.end())
    with jax.named_scope("end_b"):
        share_b.product(2)
        mid_b.begin(*share_b.end())
    with jax.named_scope("end_v"):
        share_v.far()
        for slot in (0, 3, 1, 2):
            share_v.product(slot)
        mid_v.begin(*share_v.end())
    with jax.named_scope("end_z"):
        mid_z.begin(*ring_z.end())
    with jax.named_scope("gt1"):
        lax.fori_loop(0, 4, grad_tokens, 0)
    with jax.named_scope("mid_a"):
        end_a.begin(*mid_a.halves())
    with jax.named_scope("mid_b"):
        end_b.begin(*mid_b.halves())
    with jax.named_scope("mid_v"):
        end_v.begin(*mid_v.halves())
    with jax.named_scope("mid_z"):
        end_z.begin(*mid_z.halves())
    with jax.named_scope("gt2"):
        lax.fori_loop(4, 8, grad_tokens, 0)
    gw = r.gw_out
    with jax.named_scope("finish"):
        gw[:, :WA] = end_a.end()
        gw[:, WA + WZ : WA + WZ + WB] = end_b.end()
        gw[:, WA + WZ + WB :] = end_v.end()
        gw[:, WA : WA + WZ] = end_z.end()
    with jax.named_scope("drain"):
        for part in (gather, share_a, share_b, share_v, ring_z, mid_a, mid_b, mid_v, mid_z, end_a, end_b, end_v, end_z):
            part.end() if part is gather else part.drain()
        sent(dr.at[pl.ds(0, 15)], r.s_scan.at[0], mate)
        for n, l in ((0, r.ly), (1, r.lx)):
            sent(l.at[pl.ds(1, 3)], r.t_sem.at[n], mate)
        for kind in range(2):
            sent(rmsg.at[kind, pl.ds(0, 15)], r.s_scan.at[1 + kind], mate)
            sent(rres.at[kind, pl.ds(0, 15)], r.s_scan.at[3 + kind], mate)
        for copy in copies:
            copy.wait_send()


def fused(tokens, w, a_log, dt_bias, d_skip, grad_y):
    count = tokens.shape[0]
    cols, depth = w.shape
    sd = jax.ShapeDtypeStruct
    dma = pltpu.SemaphoreType.DMA
    scratch = dict(
        tok=((count, 2048), BF16), g=((count, INNER), BF16), wbuf=((8, cols, depth), BF16), acc=((count, cols), F32),
        tt=((2, 4, 4, 64, count), F32), tt3=((2, 8, 128, count), F32),
        tb=((2, 4, 4, 64, count), BF16), tb3=((2, 8, 128, count), BF16),
        tr=((4, 4, 64, count), BF16), tr3=((8, 128, count), BF16),
        t1=((4, 256, 2 * count), BF16), t2=((4, 256, 2 * count), BF16), lx=((4, 256, 2 * count), BF16), ly=((4, 256, 2 * count), BF16), t3=((8, 128, 2 * count), BF16),
        x=((count, INNER), BF16),
        dte=((count, INNER), F32), ece=((count, INNER), F32), tle=((count, INNER), F32),
        cume=((count, 2 * INNER), F32), cumt=((128, count), F32),
        xdt=((count, INNER), BF16), xt=((count, INNER), BF16), gec=((count, INNER), BF16),
        yi=((count, INNER), F32), dxi=((count, INNER), F32), ds_acc=((128, 128), F32),
        stf=((2, 2, 128, 1024), F32), sst=((2, 128, 1024), BF16), pst=((2, 128, 1024), BF16),
        tot_s=((8, 128), F32), tot_r=((8, 128), F32), te=((2, 2, 8, 1024), F32),
        dmsg=((8, 8, 128), F32), dr=((16, 8, 128), F32),
        msg=((2, 16, 64, 128), BF16), rmsg=((2, 16, 64, 128), BF16),
        res=((2, 16, 64, 128), BF16), rres=((2, 16, 64, 128), BF16),
        se=((2, 2, 128, 1024), BF16), hs=((2, 128, 1024), BF16), ske=((8, INNER), F32),
        ga=((8, count, WA), BF16), gb=((8, count, WB), BF16), gv=((8, count, WV), BF16), gz=((2, count, WZ), BF16),
        acc_a=((256, WA), F32), acc_b=((256, WB), F32), acc_v=((256, WV), F32),
        pz=((8, 128, WZ), BF16), got_z=((16, 64, WZ), BF16),
        qa=((4, 64, WA), BF16), qb=((4, 64, WB), BF16), qv=((4, 64, WV), BF16), qz=((4, 32, WZ), BF16),
        got_a=((4, 64, WA), BF16), got_b=((4, 64, WB), BF16), got_v=((4, 64, WV), BF16), got_zx=((4, 32, WZ), BF16),
        fa_s=((8, 8, WA), BF16), fa_g=((8, 8, WA), BF16), fb_s=((8, 8, WB), BF16), fb_g=((8, 8, WB), BF16),
        fv_s=((8, 8, WV), BF16), fv_g=((8, 8, WV), BF16), fz_s=((4, 8, WZ), BF16), fz_g=((4, 8, WZ), BF16),
    )
    sems = dict(
        in_sem=(3,), tok_sem=(4,), g_send=(1,), g_ici=(7, 3), g_d2d=(7,), d_sem=(12,), s_scan=(5,), r_scan=(5,),
        t_sem=(4,), s_share=(4,), r_share=(3, 4, 2), d_share=(3, 4), rz=(16,), s_last=(8,), r_last=(8,),
    )

    def body(tokens, w, a_log, dt_bias, d_skip, grad_y, y_out, gt_out, gw_out, *rest):
        r = SimpleNamespace(**dict(zip([*scratch, *sems], rest)))
        r.tokens, r.w, r.a_log, r.dt_bias, r.d_skip, r.grad_y = tokens, w, a_log, dt_bias, d_skip, grad_y
        r.y_out, r.gt_out, r.gw_out = y_out, gt_out, gw_out
        kernel(r)

    return pl.pallas_call(
        body,
        out_shape=(pltpu.VMEM((count, INNER), BF16), pltpu.VMEM((count, 2048), BF16), pltpu.VMEM((8, cols), F32)),
        in_specs=[ANY, ANY, VM, VM, VM, ANY],
        out_specs=(VM, VM, VM),
        scratch_shapes=[pltpu.VMEM(*v) for v in scratch.values()] + [dma(v) for v in sems.values()],
        compiler_params=pltpu.CompilerParams(collective_id=0, has_side_effects=True, vmem_limit_bytes=LIMIT),
    )(tokens, w, a_log.reshape(1, -1), dt_bias.reshape(1, -1), d_skip.reshape(1, -1), grad_y)


def per_device(tokens, w_in, a_log, dt_bias, d_skip, grad_y):
    count, width = tokens.shape[1:]
    inner = grad_y.shape[2]
    y, gt, gw = fused(tokens.reshape(count, width), w_in.T, a_log, dt_bias, d_skip, grad_y.reshape(count, inner))
    return (y.reshape(1, count, inner), gt.reshape(1, count, width), gw)


def solution(mesh):
    torus = Mesh(mesh.devices.reshape(2, 8, 2, 2, 4), ("xh", "z", "c", "xl", "y"))
    placed = (P(ZERO, SEQ, None), P(ZERO, None), P(), P(), P(), P(ZERO, SEQ, None))
    return jax.shard_map(
        per_device,
        mesh=torus,
        in_specs=placed,
        out_specs=(P(ZERO, SEQ, None), P(ZERO, SEQ, None), P(SEQ + ZERO, None)),
        check_vma=False,
    )
```

time: 115 us -> 99.9 us (0.87)
  Pallas kernels: 110 us -> 96.9 us
  local copies, waits for them, and re-layouts: 3.38 us -> 2.22 us
    pallas_call x1, Pallas kernels: 110 us -> 96.9 us  [fused(): pl.pallas_call(body, out_shape=(pltpu.VMEM((count, INNER), BF16), pltpu.V...]
    unnamed x7 -> x3, local copies, waits for them, and re-layouts: 3.38 us -> 2.22 us
where the time goes in v3:
time: 99.9 us; the launch traced here: 99.8 us
  Pallas kernels  96.9 us (97%)
  local copies, waits for them, and re-layouts  2.22 us (2%)
    pallas_call x1, Pallas kernels, fused(): pl.pallas_call(body, out_shape=(pltpu.VMEM((count, INNER), BF16), pltpu.V...  96.9 us
    unnamed x3, local copies, waits for them, and re-layouts  2.22 us

profile of v3, /device:TPU:1, one launch (start us, length us, event | category | flops | bytes accessed | tf_op | source)
XLA Modules:
  0.0 99.8 jit_solution(14967489043121340620)
XLA Ops:
  0.6 96.9 %shard_map.85 = (bf16[128,2048]{1,0:T(8,128)(2,1)S(1)}, bf16[128,2048]{1,0:T(8,128)(2,1)S(1)}, f32[8,2336]{1,0:T(8,128)S(1)}) custom-call(bf16[128,2048]{1,0:T(8,128)(2,1)} %bitcast.11, bf16[2336,256]{1,0:T(8,128)(2,1)} %bitcast.10, f32[1,32]{1,0:T(1,128)} %bitcast.13, f32[1,32]{1,0:T(1,128)} %bitcast.14, f32[1,32]{1,0:T(1,128)} %bitcast.15, ...), custom_call_target="tpu_custom_call" | custom-call | tf_op jit(solution)/shard_map/pallas_call | solution.py:798
  97.6 0.8 copy.12
  98.4 0.8 copy.13
  99.2 0.6 copy.14

commit v4 on v3

--- a/solution.py
+++ b/solution.py
@@ -18,7 +18,8 @@
 ANY = pl.BlockSpec(memory_space=pl.ANY)
 INNER = 2048
 EDGE_SMALL, EDGE_LARGE = 384, 400
-WA, WZ, WB, WV = 1024, 384, 768, 160
+WA, WZ, WB, WV = 896, 512, 768, 160
+PARTS = ((0, 0, 512), (0, 512, 896), (1, 0, 384), (1, 384, 768), (2, 0, 160))
 
 
 def remote(src, dst, send, recv, target):
@@ -199,9 +200,9 @@
         value = dot(self.lhs[slot], rhs)
         self.acc[...] = value if slot == 0 else self.acc[...] + value
 
-    def end(self):
+    def end(self, lo, hi):
         h = self.acc.shape[0] // 2
-        return self.acc[:h], self.acc[h:]
+        return self.acc[:h, lo:hi], self.acc[h:, lo:hi]
 
     def drain(self):
         sent(self.g.at[pl.ds(0, 7)], self.sem, self.mate)
@@ -368,6 +369,9 @@
     with jax.named_scope("g3"):
         ga(2, (at.left, 6))
         gb(2, (at.right, 6))
+        swap.wait()
+        swap3.wait()
+        place_rows(128, tr[...], tr3[...])
         gb(4)
         ga(5)
         gather.whole(0)
@@ -378,6 +382,12 @@
         gm(4)
         ga(6)
         gb(6)
+        by_y = [(d, (y + d) % 4, {"y": (y + d) % 4}) for d in (2, 1, 3)]
+        by_x = [(d, (x + d) % 4, along_x((x + d) % 4)) for d in (2, 1, 3)]
+        for n, (t, l, me, targets) in enumerate(((t2, r.ly, y, by_y), (t1, r.lx, x, by_x))):
+            for d, to, target in targets:
+                remote(t.at[to], l.at[4 - d], r.t_sem.at[n], r.t_sem.at[2 + n], target).start()
+            l[0] = t[me]
         gm(2)
         gm(5)
         gather.whole(1)
@@ -389,11 +399,10 @@
         gather.whole(5)
         multiply(rel[2], rel[5])
     with jax.named_scope("g6"):
-        swap.wait()
-        swap3.wait()
         gather.whole(6)
+    last_tok = tok[:, pl.ds(pl.multiple_of(rel[6] * depth, depth), depth)]
     with jax.named_scope("g7"):
-        multiply(rel[6])
+        acc[:, INNER:] += dot_nt(last_tok, wbuf[rel[6], INNER:])
 
     x_r, g_r = r.x, r.g
     dte, ece, tle, cume, cumt = r.dte, r.ece, r.tle, r.cume, r.cumt
@@ -446,7 +455,7 @@
         st_b = local_states(1, ct, gec)
         widen(dt, dte)
         widen(jnp.exp(total - cum), tle)
-        xs = acc[:, :INNER].astype(BF16)
+        xs = (acc[:, :INNER] + dot_nt(last_tok, wbuf[rel[6], :INNER])).astype(BF16)
         x_r[...] = xs
         xd = xs.astype(F32) * dte[...]
         xdt[...] = xd.astype(BF16)
@@ -514,9 +523,6 @@
 
     with jax.named_scope("send_b"):
         send_states(1)
-    with jax.named_scope("send_f"):
-        send_states(0)
-
     with jax.named_scope("pairs_prep"):
         cumt[...] = cum.T
         scores = dot_nt(cm, bm)
@@ -549,19 +555,14 @@
         dxi[:, cols] = dot(jnp.concatenate(mix_t, axis=1), gg)
         return carry
 
-    by_y = [(d, (y + d) % 4, {"y": (y + d) % 4}) for d in (2, 1, 3)]
-    by_x = [(d, (x + d) % 4, along_x((x + d) % 4)) for d in (2, 1, 3)]
     with jax.named_scope("pairs1"):
-        place_rows(128, tr[...], tr3[...])
-        for n, (t, l, me, targets) in enumerate(((t2, r.ly, y, by_y), (t1, r.lx, x, by_x))):
-            for d, to, target in targets:
-                remote(t.at[to], l.at[4 - d], r.t_sem.at[n], r.t_sem.at[2 + n], target).start()
-            l[0] = t[me]
-        lax.fori_loop(0, 6, pair, 0)
+        lax.fori_loop(0, 5, pair, 0)
+    with jax.named_scope("send_f"):
+        send_states(0)
     with jax.named_scope("scan_b"):
         scan_states(1)
     with jax.named_scope("pairs2"):
-        lax.fori_loop(6, 11, pair, 0)
+        lax.fori_loop(5, 11, pair, 0)
     with jax.named_scope("scan_f"):
         scan_states(0)
     with jax.named_scope("pairs3"):
@@ -598,11 +599,14 @@
         dxs = tle[:, cols] * dot(bm, en)
         dxn = dxi[:, cols] + dxs
         dx = (dte[:, cols] * dxn + ske[0:1, cols] * g_r[:, cols].astype(F32)).astype(BF16)
-        if q < 2:
-            ga[0, :, q * 512 : q * 512 + 512] = dx
+        if q == 0:
+            ga[0, :, :512] = dx
+        elif q == 1:
+            ga[0, :, 512:] = dx[:, :384]
+            gz[0, :, :128] = dx[:, 384:]
         elif q == 2:
-            gz[0, :, :] = dx[:, :WZ]
-            gb[0, :, :128] = dx[:, WZ:]
+            gz[0, :, 128:] = dx[:, :384]
+            gb[0, :, :128] = dx[:, 384:]
         else:
             gb[0, :, 128:640] = dx
         p2.append(heads(xs * dxn, segment))
@@ -702,48 +706,62 @@
     def scatter(n, me, targets, src, got):
         return Scatter(me, targets, src, got, r.s_last.at[n], r.r_last.at[n])
 
-    mid_a = scatter(0, x, by_x, r.qa, r.got_a)
-    mid_b = scatter(1, y, by_y, r.qb, r.got_b)
-    mid_v = scatter(2, x, by_x, r.qv, r.got_v)
-    mid_z = scatter(3, x, by_x, r.qz, r.got_zx)
-    end_a = scatter(4, z, by_z, r.fa_s, r.fa_g)
-    end_b = scatter(5, z, by_z, r.fb_s, r.fb_g)
-    end_v = scatter(6, z, by_z, r.fv_s, r.fv_g)
-    end_z = scatter(7, y, by_y, r.fz_s, r.fz_g)
+    shares = ((share_a, x, by_x, 0), (share_b, y, by_y, WA + WZ), (share_v, x, by_x, WA + WZ + WB))
+    stages = []
+    for n, (k, lo, hi) in enumerate(PARTS):
+        q, got, fs, fg = r.extra[4 * n : 4 * n + 4]
+        share, me, targets, base = shares[k]
+        mid, end = scatter(2 * n, me, targets, q, got), scatter(2 * n + 1, z, by_z, fs, fg)
+        stages.append((mid, end, share, lo, hi, base))
+    mid_z = scatter(10, x, by_x, r.qz, r.got_zx)
+    end_z = scatter(11, y, by_y, r.fz_s, r.fz_g)
+
+    def enter(n):
+        mid, end, share, lo, hi, base = stages[n]
+        mid.begin(*share.end(lo, hi))
+
     with jax.named_scope("end_a"):
         share_a.product(2)
-        mid_a.begin(*share_a.end())
+        enter(0)
+        enter(1)
     with jax.named_scope("end_b"):
         share_b.product(2)
-        mid_b.begin(*share_b.end())
+        enter(2)
+        enter(3)
     with jax.named_scope("end_v"):
         share_v.far()
         for slot in (0, 3, 1, 2):
             share_v.product(slot)
-        mid_v.begin(*share_v.end())
+        enter(4)
     with jax.named_scope("end_z"):
         mid_z.begin(*ring_z.end())
     with jax.named_scope("gt1"):
         lax.fori_loop(0, 4, grad_tokens, 0)
-    with jax.named_scope("mid_a"):
-        end_a.begin(*mid_a.halves())
-    with jax.named_scope("mid_b"):
-        end_b.begin(*mid_b.halves())
+    with jax.named_scope("mid_1"):
+        for n in (0, 2):
+            stages[n][1].begin(*stages[n][0].halves())
+    with jax.named_scope("mid_2"):
+        for n in (1, 3):
+            stages[n][1].begin(*stages[n][0].halves())
     with jax.named_scope("mid_v"):
-        end_v.begin(*mid_v.halves())
+        stages[4][1].begin(*stages[4][0].halves())
     with jax.named_scope("mid_z"):
         end_z.begin(*mid_z.halves())
     with jax.named_scope("gt2"):
         lax.fori_loop(4, 8, grad_tokens, 0)
     gw = r.gw_out
     with jax.named_scope("finish"):
-        gw[:, :WA] = end_a.end()
-        gw[:, WA + WZ : WA + WZ + WB] = end_b.end()
-        gw[:, WA + WZ + WB :] = end_v.end()
+        for n in (0, 2, 1, 3, 4):
+            mid, end, share, lo, hi, base = stages[n]
+            gw[:, base + lo : base + hi] = end.end()
         gw[:, WA : WA + WZ] = end_z.end()
     with jax.named_scope("drain"):
-        for part in (gather, share_a, share_b, share_v, ring_z, mid_a, mid_b, mid_v, mid_z, end_a, end_b, end_v, end_z):
-            part.end() if part is gather else part.drain()
+        gather.end()
+        for part in (share_a, share_b, share_v, ring_z, mid_z, end_z):
+            part.drain()
+        for mid, end, *rest in stages:
+            mid.drain()
+            end.drain()
         sent(dr.at[pl.ds(0, 15)], r.s_scan.at[0], mate)
         for n, l in ((0, r.ly), (1, r.lx)):
             sent(l.at[pl.ds(1, 3)], r.t_sem.at[n], mate)
@@ -779,18 +797,20 @@
         ga=((8, count, WA), BF16), gb=((8, count, WB), BF16), gv=((8, count, WV), BF16), gz=((2, count, WZ), BF16),
         acc_a=((256, WA), F32), acc_b=((256, WB), F32), acc_v=((256, WV), F32),
         pz=((8, 128, WZ), BF16), got_z=((16, 64, WZ), BF16),
-        qa=((4, 64, WA), BF16), qb=((4, 64, WB), BF16), qv=((4, 64, WV), BF16), qz=((4, 32, WZ), BF16),
-        got_a=((4, 64, WA), BF16), got_b=((4, 64, WB), BF16), got_v=((4, 64, WV), BF16), got_zx=((4, 32, WZ), BF16),
-        fa_s=((8, 8, WA), BF16), fa_g=((8, 8, WA), BF16), fb_s=((8, 8, WB), BF16), fb_g=((8, 8, WB), BF16),
-        fv_s=((8, 8, WV), BF16), fv_g=((8, 8, WV), BF16), fz_s=((4, 8, WZ), BF16), fz_g=((4, 8, WZ), BF16),
+        qz=((4, 32, WZ), BF16), got_zx=((4, 32, WZ), BF16), fz_s=((4, 8, WZ), BF16), fz_g=((4, 8, WZ), BF16),
     )
     sems = dict(
         in_sem=(3,), tok_sem=(4,), g_send=(1,), g_ici=(7, 3), g_d2d=(7,), d_sem=(12,), s_scan=(5,), r_scan=(5,),
-        t_sem=(4,), s_share=(4,), r_share=(3, 4, 2), d_share=(3, 4), rz=(16,), s_last=(8,), r_last=(8,),
+        t_sem=(4,), s_share=(4,), r_share=(3, 4, 2), d_share=(3, 4), rz=(16,), s_last=(12,), r_last=(12,),
     )
+
+    extra = []
+    for k, lo, hi in PARTS:
+        extra += [pltpu.VMEM((4, 64, hi - lo), BF16)] * 2 + [pltpu.VMEM((8, 8, hi - lo), BF16)] * 2
 
     def body(tokens, w, a_log, dt_bias, d_skip, grad_y, y_out, gt_out, gw_out, *rest):
         r = SimpleNamespace(**dict(zip([*scratch, *sems], rest)))
+        r.extra = rest[len(scratch) + len(sems) :]
         r.tokens, r.w, r.a_log, r.dt_bias, r.d_skip, r.grad_y = tokens, w, a_log, dt_bias, d_skip, grad_y
         r.y_out, r.gt_out, r.gw_out = y_out, gt_out, gw_out
         kernel(r)
@@ -800,7 +820,7 @@
         out_shape=(pltpu.VMEM((count, INNER), BF16), pltpu.VMEM((count, 2048), BF16), pltpu.VMEM((8, cols), F32)),
         in_specs=[ANY, ANY, VM, VM, VM, ANY],
         out_specs=(VM, VM, VM),
-        scratch_shapes=[pltpu.VMEM(*v) for v in scratch.values()] + [dma(v) for v in sems.values()],
+        scratch_shapes=[pltpu.VMEM(*v) for v in scratch.values()] + [dma(v) for v in sems.values()] + extra,
         compiler_params=pltpu.CompilerParams(collective_id=0, has_side_effects=True, vmem_limit_bytes=LIMIT),
     )(tokens, w, a_log.reshape(1, -1), dt_bias.reshape(1, -1), d_skip.reshape(1, -1), grad_y)
 

time: 99.9 us -> 97 us (0.971)
  Pallas kernels: 96.9 us -> 94 us
    pallas_call x1, Pallas kernels: 96.9 us -> 94 us  [fused(): pl.pallas_call(body, out_shape=(pltpu.VMEM((count, INNER), BF16), pltpu.V...]
where the time goes in v4:
time: 97 us; the launch traced here: 96.9 us
  Pallas kernels  94 us (97%)
  local copies, waits for them, and re-layouts  2.22 us (2%)
    pallas_call x1, Pallas kernels, fused(): pl.pallas_call(body, out_shape=(pltpu.VMEM((count, INNER), BF16), pltpu.V...  94 us
    unnamed x3, local copies, waits for them, and re-layouts  2.22 us

profile of v4, /device:TPU:1, one launch (start us, length us, event | category | flops | bytes accessed | tf_op | source)
XLA Modules:
  0.0 96.9 jit_solution(10948873132349348773)
XLA Ops:
  0.6 94.0 %shard_map.85 = (bf16[128,2048]{1,0:T(8,128)(2,1)S(1)}, bf16[128,2048]{1,0:T(8,128)(2,1)S(1)}, f32[8,2336]{1,0:T(8,128)S(1)}) custom-call(bf16[128,2048]{1,0:T(8,128)(2,1)} %bitcast.11, bf16[2336,256]{1,0:T(8,128)(2,1)} %bitcast.10, f32[1,32]{1,0:T(1,128)} %bitcast.13, f32[1,32]{1,0:T(1,128)} %bitcast.14, f32[1,32]{1,0:T(1,128)} %bitcast.15, ...), custom_call_target="tpu_custom_call" | custom-call | tf_op jit(solution)/shard_map/pallas_call | solution.py:818
  94.6 0.8 copy.12
  95.4 0.8 copy.13
  96.2 0.6 copy.14

commit v5 on v4

--- a/solution.py
+++ b/solution.py
@@ -825,10 +825,29 @@
     )(tokens, w, a_log.reshape(1, -1), dt_bias.reshape(1, -1), d_skip.reshape(1, -1), grad_y)
 
 
+def leave_kernel(*refs):
+    copies = [pltpu.make_async_copy(refs[n], refs[3 + n], refs[6].at[n]) for n in range(3)]
+    for copy in copies:
+        copy.start()
+    for copy in copies:
+        copy.wait()
+
+
+def leave(*arrays):
+    return pl.pallas_call(
+        leave_kernel,
+        out_shape=tuple(jax.ShapeDtypeStruct(a.shape, a.dtype) for a in arrays),
+        in_specs=[VM] * 3,
+        out_specs=(ANY,) * 3,
+        scratch_shapes=[pltpu.SemaphoreType.DMA((3,))],
+    )(*(pltpu.with_memory_space_constraint(a, pltpu.VMEM) for a in arrays))
+
+
 def per_device(tokens, w_in, a_log, dt_bias, d_skip, grad_y):
     count, width = tokens.shape[1:]
     inner = grad_y.shape[2]
     y, gt, gw = fused(tokens.reshape(count, width), w_in.T, a_log, dt_bias, d_skip, grad_y.reshape(count, inner))
+    y, gt, gw = leave(y, gt, gw)
     return (y.reshape(1, count, inner), gt.reshape(1, count, width), gw)
 
 

time: 97 us -> 95.8 us (0.988)
  local copies, waits for them, and re-layouts: 2.22 us -> 0 us
  Pallas kernels: 94 us -> 95 us
    unnamed x3 -> x0, local copies, waits for them, and re-layouts: 2.22 us -> none
    pallas_call x0 -> x1, Pallas kernels: none -> 1.01 us  [leave(): pl.pallas_call(leave_kernel, out_shape=tuple((jax.ShapeDtypeStruct(a.shap...]
where the time goes in v5:
time: 95.8 us; the launch traced here: 95.7 us
  Pallas kernels  95 us (99%)
    pallas_call x1, Pallas kernels, fused(): pl.pallas_call(body, out_shape=(pltpu.VMEM((count, INNER), BF16), pltpu.V...  94 us

profile of v5, /device:TPU:1, one launch (start us, length us, event | category | flops | bytes accessed | tf_op | source)
XLA Modules:
  0.0 95.7 jit_solution(2769451912371269658)
XLA Ops:
  0.6 94.0 %shard_map.85 = (bf16[128,2048]{1,0:T(8,128)(2,1)S(1)}, bf16[128,2048]{1,0:T(8,128)(2,1)S(1)}, f32[8,2336]{1,0:T(8,128)S(1)}) custom-call(bf16[128,2048]{1,0:T(8,128)(2,1)} %bitcast.9, bf16[2336,256]{1,0:T(8,128)(2,1)} %bitcast.8, f32[1,32]{1,0:T(1,128)} %bitcast.11, f32[1,32]{1,0:T(1,128)} %bitcast.12, f32[1,32]{1,0:T(1,128)} %bitcast.13, ...), custom_call_target="tpu_custom_call" | custom-call | tf_op jit(solution)/shard_map/pallas_call | solution.py:818
  94.6 1.0 %shard_map.86 = (bf16[128,2048]{1,0:T(8,128)(2,1)}, bf16[128,2048]{1,0:T(8,128)(2,1)}, f32[8,2336]{1,0:T(8,128)}) custom-call(bf16[128,2048]{1,0:T(8,128)(2,1)S(1)} %get-tuple-element.9.refs_0_, bf16[128,2048]{1,0:T(8,128)(2,1)S(1)} %get-tuple-element.10.refs_1_, f32[8,2336]{1,0:T(8,128)S(1)} %get-tuple-element.11.refs_2_), custom_call_target="tpu_custom_call" | custom-call | tf_op jit(solution)/shard_map/pallas_call | solution.py:837

commit v6 on v5

--- a/solution.py
+++ b/solution.py
@@ -457,11 +457,7 @@
         widen(jnp.exp(total - cum), tle)
         xs = (acc[:, :INNER] + dot_nt(last_tok, wbuf[rel[6], :INNER])).astype(BF16)
         x_r[...] = xs
-        xd = xs.astype(F32) * dte[...]
-        xdt[...] = xd.astype(BF16)
-        xt[...] = (xd * tle[...]).astype(BF16)
-        bt = bm.astype(F32).T.astype(BF16)
-        st_copies = [local_states(0, bt, xt), st_b]
+        st_copies = [None, st_b]
         tot_copy.wait()
         for n, arr in enumerate((tot_s, tot_r)):
             for j, e in enumerate(spread(arr[...])):
@@ -523,6 +519,11 @@
 
     with jax.named_scope("send_b"):
         send_states(1)
+        xd = x_r[...].astype(F32) * dte[...]
+        xdt[...] = xd.astype(BF16)
+        xt[...] = (xd * tle[...]).astype(BF16)
+        bt = bm.astype(F32).T.astype(BF16)
+        st_copies[0] = local_states(0, bt, xt)
     with jax.named_scope("pairs_prep"):
         cumt[...] = cum.T
         scores = dot_nt(cm, bm)
@@ -695,9 +696,9 @@
             share_a.product(slot)
             share_b.product(slot)
     with jax.named_scope("far"):
-        share_v.early()
         share_a.far()
         share_b.far()
+        share_v.early()
         ring_z.short(1)
         share_v.near()
         ring_z.long(1)

time: 95.8 us -> 94.9 us (level)
  no operation moved by 1% of the time
where the time goes in v6:
time: 94.9 us; the launch traced here: 94.8 us
  Pallas kernels  94.1 us (99%)
    pallas_call x1, Pallas kernels, fused(): pl.pallas_call(body, out_shape=(pltpu.VMEM((count, INNER), BF16), pltpu.V...  93.1 us

profile of v6, /device:TPU:1, one launch (start us, length us, event | category | flops | bytes accessed | tf_op | source)
XLA Modules:
  0.0 94.8 jit_solution(5581624645707131044)
XLA Ops:
  0.6 93.1 %shard_map.85 = (bf16[128,2048]{1,0:T(8,128)(2,1)S(1)}, bf16[128,2048]{1,0:T(8,128)(2,1)S(1)}, f32[8,2336]{1,0:T(8,128)S(1)}) custom-call(bf16[128,2048]{1,0:T(8,128)(2,1)} %bitcast.9, bf16[2336,256]{1,0:T(8,128)(2,1)} %bitcast.8, f32[1,32]{1,0:T(1,128)} %bitcast.11, f32[1,32]{1,0:T(1,128)} %bitcast.12, f32[1,32]{1,0:T(1,128)} %bitcast.13, ...), custom_call_target="tpu_custom_call" | custom-call | tf_op jit(solution)/shard_map/pallas_call | solution.py:819
  93.8 1.0 %shard_map.86 = (bf16[128,2048]{1,0:T(8,128)(2,1)}, bf16[128,2048]{1,0:T(8,128)(2,1)}, f32[8,2336]{1,0:T(8,128)}) custom-call(bf16[128,2048]{1,0:T(8,128)(2,1)S(1)} %get-tuple-element.9.refs_0_, bf16[128,2048]{1,0:T(8,128)(2,1)S(1)} %get-tuple-element.10.refs_1_, f32[8,2336]{1,0:T(8,128)S(1)} %get-tuple-element.11.refs_2_), custom_call_target="tpu_custom_call" | custom-call | tf_op jit(solution)/shard_map/pallas_call | solution.py:838
